TPU v7x, 256 devices: a whole 4x4x8 slice. The times are simulated.
256 devices in a mesh: gx: 8 (over x, core), gy: 4 (over z_hi), gz: 8 (over z_lo, y).
Axes of the slice: x: 4, y: 4, z: 8 (z_hi: 4, z_lo: 2; z = z_hi * 2 + z_lo), core: 2. Of those that a mesh axis runs over, the one named last changes fastest.
Arguments:
- hidden_rows: bfloat16 [4096, 16384], P(('gx', 'gy'), 'gz'), may hold values from -2000 to 2000
- norm_gain: bfloat16 [16384], P('gz'), may hold values from 0.5 to 1.5
- w_query: bfloat16 [16384, 16384], P('gz', ('gx', 'gy')), may hold values from -0.046875 to 0.046875
- w_keyval: bfloat16 [16384, 2048], P('gz', ('gx', 'gy')), may hold values from -0.046875 to 0.046875
- positions: int32 [4096], P('gz'), may hold values from 0 to 1023, as said below
- keyval_order: int32 [8], replicated, may hold values from 0 to 7, each once
Outputs:
- queries: bfloat16 [4096, 16384], P('gz', ('gx', 'gy'))
- keyval_owned: bfloat16 [8, 4096, 256], P('gy', 'gz')
Inputs may be any that keep to these rules, and one draw needn't show every extreme that they name: `positions`: each token's position within its packed document: 0 where a document starts, else one more than the previous token's; a document holds at most 1024 tokens. `keyval_order`: each head once.
All inputs are finite; a program needn't handle non-finite values.
Results may differ from a plain program's by a relative error of at most 0.0066.
Values may be sent and summed in bfloat16 or wider, within the bound.
A program may use at most 128 MiB of HBM per device.

v0:
```python
import math

import jax
import jax.numpy as jnp
from jax import lax
from jax.sharding import PartitionSpec as P

D = 16384
KVH = 8
HD = 128


rope_base = 500000.0
norm_eps = 1e-05


def from_everyone(value, axis):
    copies = jnp.broadcast_to(value, (lax.axis_size(axis), *value.shape))
    return lax.all_to_all(copies, axis, split_axis=0, concat_axis=0, tiled=True)


def taken_together(value, axis):
    everything = from_everyone(value, axis)
    return jnp.sum(everything, axis=0)


def in_blocks(value, dim, count):
    before, after = (value.shape[:dim], value.shape[dim + 1 :])
    return jnp.moveaxis(value.reshape(*before, count, -1, *after), dim, 0)


def summed_on_arrival(value, axis, dim):
    count = lax.axis_size(axis)
    blocks = lax.all_to_all(in_blocks(value, dim, count), axis, 0, 0, tiled=True)
    return jnp.sum(blocks.astype(jnp.float32), axis=0)


def rotate_pairs(values, position_ids, col_start, keys_only):
    row_total, col_width = values.shape
    pair_col = col_start + 2 * jnp.arange(col_width // 2, dtype=jnp.int32)
    within = pair_col % HD
    inv_freq = jnp.exp((within // 2).astype(jnp.float32) * (-2.0 * math.log(rope_base) / HD))
    angles = position_ids.astype(jnp.float32)[:, None] * inv_freq[None, :]
    cosines = jnp.cos(angles)
    sine_part = jnp.sin(angles)
    paired = values.reshape(row_total, col_width // 2, 2)
    even_part = paired[..., 0]
    odd_part = paired[..., 1]
    rotated = jnp.stack(
        [even_part * cosines - odd_part * sine_part, even_part * sine_part + odd_part * cosines],
        axis=-1,
    )
    if keys_only:
        is_key = (pair_col // HD % 2 == 0)[None, :, None]
        rotated = jnp.where(is_key, rotated, paired)
    return rotated.reshape(row_total, col_width)


def body(hidden_rows, norm_gain, w_query, w_keyval, positions, keyval_order):
    widened_gain = norm_gain.astype(jnp.float32)
    widened = hidden_rows.astype(jnp.float32)
    factor = lax.rsqrt(taken_together(jnp.sum(widened * widened, axis=1), "gz") / D + norm_eps)
    normed_rows = (
        hidden_rows.astype(jnp.float32) * factor[:, None] * widened_gain[None, :]
    ).astype(jnp.bfloat16)
    query_width = w_query.shape[1]
    keyval_width = w_keyval.shape[1]
    group_size = lax.axis_size("gy")
    gathered = lax.all_gather(normed_rows, ("gx", "gy"), axis=0, tiled=True)
    query_sum = summed_on_arrival(
        jnp.dot(gathered, w_query, preferred_element_type=jnp.float32).astype(jnp.bfloat16), "gz", 0
    )
    keyval_sum = summed_on_arrival(
        jnp.dot(gathered, w_keyval, preferred_element_type=jnp.float32).astype(jnp.bfloat16),
        "gz",
        0,
    )
    col_index = lax.axis_index("gx") * group_size + lax.axis_index("gy")
    queries = rotate_pairs(query_sum, positions, col_index * query_width, False).astype(
        jnp.bfloat16
    )
    keyval_part = rotate_pairs(keyval_sum, positions, col_index * keyval_width, True).astype(
        jnp.bfloat16
    )
    keyval_all = lax.all_gather(keyval_part, ("gx", "gy"), axis=1, tiled=True)
    slot_count = KVH // group_size
    first_slot = lax.axis_index("gy") * slot_count
    keyval_heads = keyval_all.reshape(keyval_all.shape[0], KVH, 2 * HD)
    wanted = lax.dynamic_slice_in_dim(keyval_order, first_slot, slot_count, 0)
    selector = (wanted[:, None] == jnp.arange(KVH, dtype=jnp.int32)[None, :]).astype(jnp.bfloat16)
    keyval_owned = jnp.einsum(
        "sh,rhc->src", selector, keyval_heads, preferred_element_type=jnp.float32
    ).astype(jnp.bfloat16)
    return (queries, keyval_owned)


def solution(mesh):
    in_specs = (
        P(("gx", "gy"), "gz"),
        P("gz"),
        P("gz", ("gx", "gy")),
        P("gz", ("gx", "gy")),
        P("gz"),
        P(),
    )
    out_specs = (P("gz", ("gx", "gy")), P("gy", "gz", None))
    return jax.shard_map(body, mesh=mesh, in_specs=in_specs, out_specs=out_specs, check_vma=False)
```

profile of v0, /device:TPU:1, one launch (start us, length us, event | category | flops | bytes accessed | tf_op | source)
XLA Modules:
  0.0 268.1 jit_solution(16777390107375378753)
XLA Ops:
  7.2 1.4 fusion
  8.6 0.6 broadcast_in_dim.14
  9.2 6.4 %all-to-all-start = ((f32[8,1,128]{2,1,0:T(1,128)}), f32[8,1,128]{2,1,0:T(1,128)S(1)}, u32[]{:S(2)}, u32[]{:S(2)}) async-start(f32[8,1,128]{2,1,0:T(1,128)} %broadcast_in_dim.14), calls=%async_computation | async-start | bytes 8192 | tf_op jit(solution)/shard_map/all_to_all | solution.py:19
  15.6 0.7 convert_element_type.52
  16.3 4.2 %all-to-all-done = f32[8,1,128]{2,1,0:T(1,128)S(1)} async-done(((f32[8,1,128]{2,1,0:T(1,128)}), f32[8,1,128]{2,1,0:T(1,128)S(1)}, u32[]{:S(2)}, u32[]{:S(2)}) %all-to-all-start) | async-done | bytes 4128 | tf_op jit(solution)/shard_map/all_to_all | solution.py:19
  20.5 2.0 fusion.2
  22.6 107.4 %all-gather.3.cloned.1.call-done = bf16[4096,2048]{1,0:T(8,128)(2,1)} async-done(((bf16[128,2048]{1,0:T(8,128)(2,1)}), bf16[4096,2048]{1,0:T(8,128)(2,1)}) %all-gather.3.cloned.1.call-update) | async-done | bytes 16777232 | tf_op jit(solution)/shard_map/all_gather | solution.py:69
  130.0 10.9 %convolution_convert_fusion.1 = bf16[4096,64]{0,1:T(8,128)(2,1)S(1)} fusion(bf16[4096,2048]{1,0:T(8,128)(2,1)} %all-gather.3.cloned.1.call-done, bf16[2048,64]{0,1:T(8,128)(2,1)} %param.9), kind=kOutput, calls=%fused_computation.2 | convolution fusion | flops 1074003968 | bytes 17563648 | tf_op jit(solution)/shard_map/dot_general | solution.py:74
  140.9 0.8 copy.51
  141.8 18.8 %all-to-all-start.2 = ((bf16[8,512,64]{1,2,0:T(8,128)(2,1)}), bf16[8,512,64]{1,2,0:T(8,128)(2,1)S(1)}, u32[]{:S(2)}, u32[]{:S(2)}) async-start(bf16[8,512,64]{1,2,0:T(8,128)(2,1)} %bitcast.22), calls=%async_computation.2 | async-start | bytes 1048576 | tf_op jit(solution)/shard_map/all_to_all | solution.py:34
  160.6 13.7 %convolution_convert_fusion = bf16[4096,512]{1,0:T(8,128)(2,1)} fusion(bf16[4096,2048]{1,0:T(8,128)(2,1)} %all-gather.3.cloned.1.call-done, bf16[2048,512]{1,0:T(8,128)(2,1)S(1)} %copy-done), kind=kOutput, calls=%fused_computation.1 | convolution fusion | flops 8592031744 | bytes 23068672 | tf_op jit(solution)/shard_map/dot_general | solution.py:71
  174.4 5.3 %all-to-all-start.1 = ((bf16[8,512,512]{2,1,0:T(8,128)(2,1)}), bf16[8,512,512]{2,1,0:T(8,128)(2,1)}, u32[]{:S(2)}, u32[]{:S(2)}) async-start(bf16[8,512,512]{2,1,0:T(8,128)(2,1)} %bitcast.23), calls=%async_computation.1 | async-start | bytes 8388608 | tf_op jit(solution)/shard_map/all_to_all | solution.py:34
  179.6 0.2 all-gather.5.cloned.1.call-start
  180.0 0.1 broadcast_in_dim.26
  180.3 0.1 fusion.25
  180.4 0.3 fusion.15
  180.9 0.7 select_convert_fusion
  181.6 0.1 dynamic_slice.3
  181.7 57.3 %all-gather.5.cloned.1.call-done = bf16[512,2048]{0,1:T(8,128)(2,1)} async-done(((bf16[512,64]{0,1:T(8,128)(2,1)}), bf16[512,2048]{0,1:T(8,128)(2,1)}) %all-gather.5.cloned.1.call-update) | async-done | bytes 2097168 | tf_op jit(solution)/shard_map/all_gather | solution.py:85
  239.0 4.6 %copy.40 = bf16[512,8,256]{2,1,0:T(8,128)(2,1)} copy(bf16[512,8,256]{0,2,1:T(8,128)(2,1)} %bitcast.25) | data formatting | bytes 4194304 | tf_op jit(solution)/shard_map/reshape | solution.py:88
  243.6 2.3 convolution_convert_fusion.2
  245.9 0.9 copy.39
  246.8 2.9 %convert_reduce_fusion = f32[512,512]{1,0:T(8,128)S(1)} fusion(bf16[8,512,512]{2,1,0:T(8,128)(2,1)} %all-to-all-done.1), kind=kLoop, calls=%fused_computation | loop fusion | flops 3932160 | bytes 5242880 | tf_op jit(solution)/shard_map/reduce_sum | solution.py:35
  249.7 1.3 copy.29
  251.0 1.8 reshape.312
  252.8 1.8 fusion.24
  254.6 1.2 copy.41
  255.9 1.2 copy.42
  257.1 2.4 fusion.8
  259.5 0.5 copy.32
  260.1 0.2 convert_element_type.58
  260.3 1.0 copy.38
  (24 shorter events, 0.6 us)
Async XLA Ops:
  7.2 153.5 %copy-start = (bf16[2048,512]{1,0:T(8,128)(2,1)S(1)}, bf16[2048,512]{1,0:T(8,128)(2,1)}, u32[]{:S(2)}) copy-start(bf16[2048,512]{1,0:T(8,128)(2,1)} %param.8) | copy-start | bytes 6291460
  9.2 11.3 %all-to-all-start = ((f32[8,1,128]{2,1,0:T(1,128)}), f32[8,1,128]{2,1,0:T(1,128)S(1)}, u32[]{:S(2)}, u32[]{:S(2)}) async-start(f32[8,1,128]{2,1,0:T(1,128)} %broadcast_in_dim.14), calls=%async_computation | async-start | bytes 8192 | tf_op jit(solution)/shard_map/all_to_all | solution.py:19
  15.5 114.5 %all-gather.3.cloned.1.call-start = ((), (), s32[]{:S(2)}) async-start(), calls=%async_computation.3 | async-start | bytes 17301504 | tf_op jit(solution)/shard_map/all_gather | solution.py:69
  141.8 32.6 %all-to-all-start.2 = ((bf16[8,512,64]{1,2,0:T(8,128)(2,1)}), bf16[8,512,64]{1,2,0:T(8,128)(2,1)S(1)}, u32[]{:S(2)}, u32[]{:S(2)}) async-start(bf16[8,512,64]{1,2,0:T(8,128)(2,1)} %bitcast.22), calls=%async_computation.2 | async-start | bytes 1048576 | tf_op jit(solution)/shard_map/all_to_all | solution.py:34
  174.4 5.5 %copy-start.1 = (s32[512]{0:T(512)S(1)}, s32[512]{0:T(512)}, u32[]{:S(2)}) copy-start(s32[512]{0:T(512)} %param.10) | copy-start | bytes 6148
  174.4 7.3 %copy-start.2 = (s32[8]{0:T(128)S(1)}, s32[8]{0:T(128)}, u32[]{:S(2)}) copy-start(s32[8]{0:T(128)} %param.11) | copy-start | bytes 100
  174.4 72.4 %all-to-all-start.1 = ((bf16[8,512,512]{2,1,0:T(8,128)(2,1)}), bf16[8,512,512]{2,1,0:T(8,128)(2,1)}, u32[]{:S(2)}, u32[]{:S(2)}) async-start(bf16[8,512,512]{2,1,0:T(8,128)(2,1)} %bitcast.23), calls=%async_computation.1 | async-start | bytes 8388608 | tf_op jit(solution)/shard_map/all_to_all | solution.py:34
  179.6 59.4 %all-gather.5.cloned.1.call-start = ((), (), s32[]{:S(2)}) async-start(), calls=%async_computation.4 | async-start | bytes 2162688 | tf_op jit(solution)/shard_map/all_gather | solution.py:85
Sparse Core Ops, SparseCore 0:
  22.7 107.2 all-gather.2
  183.6 55.3 all-gather.4
where the time goes:
time: 269 us; the launch traced here: 268 us
  waiting for transfers between devices  169 us (63%)
  starting transfers between devices  30.7 us (11%)
  matrix products  27 us (10%)
  local copies, waits for them, and re-layouts  16.5 us (6%)
  between operations  14.2 us (5%)
  other arithmetic  10.6 us (4%)
    all_gather x1, waiting for transfers between devices, body(): gathered = lax.all_gather(normed_rows, ('gx', 'gy'), axis=0, tiled=True)  107 us
    all_gather x1, waiting for transfers between devices, body(): keyval_all = lax.all_gather(keyval_part, ('gx', 'gy'), axis=1, tiled=True)  57.3 us
    all_to_all x2, starting transfers between devices, summed_on_arrival(): lax.all_to_all(in_blocks(value, dim, count), axis, 0, 0, tiled=True)  24.1 us
    dot_general x1, matrix products, body(): jnp.dot(gathered, w_query, preferred_element_type=jnp.float32)  13.7 us
    dot_general x1, matrix products, body(): jnp.dot(gathered, w_keyval, preferred_element_type=jnp.float32)  10.9 us
    all_to_all x1, starting transfers between devices, from_everyone(): return lax.all_to_all(copies, axis, split_axis=0, concat_axis=0, tiled=True)  6.36 us
  transfers between devices with their start and end apart: 5, of which 3 were waited for; matrix products, arithmetic and copies ran while one was open for 9% of the time, Pallas kernels for 0%

commit v1 on v0

v1 whole, which is shorter than its diff:
```python
import functools
import math

import jax
import jax.numpy as jnp
import numpy as np
from jax import lax
from jax.experimental import pallas as pl
from jax.experimental.pallas import tpu as pltpu
from jax.sharding import PartitionSpec as P

D = 16384
KVH = 8
HD = 128
rope_base = 500000.0
norm_eps = 1e-05

MESH = pl.DeviceIdType.MESH
F32 = jnp.float32
BF16 = jnp.bfloat16

O, L, R, F = 0, 3, 1, 2

STEPS = [
    ((O, O), []),
    ((L, O), [(L, O, 0), (R, O, 1), (L, O, 1), (R, O, 0), (O, L, 0), (O, R, 1)]),
    ((R, O), []),
    ((F, O), [(F, O, 0), (F, O, 1)]),
    ((O, L), [(O, L, 1), (O, R, 0)]),
    ((O, R), []),
    ((O, F), [(L, L, 0), (R, R, 1), (L, R, 1), (R, L, 0), (O, F, 0), (O, F, 1), (L, L, 1), (R, R, 0)]),
    ((L, L), [(L, R, 0), (R, L, 1)]),
    ((R, R), []),
    ((L, R), []),
    ((R, L), []),
    ((L, F), [(F, L, 0), (F, R, 1), (L, F, 0), (R, F, 1), (L, F, 1), (R, F, 0)]),
    ((R, F), []),
    ((F, L), [(F, R, 0), (F, L, 1)]),
    ((F, R), []),
    ((F, F), [(F, F, 0), (F, F, 1)]),
]
N_STEPS = len(STEPS)
LAG_RELAY, LAG_PLANE, LAG_OWNER = 2, 4, 6

KV_EVENTS = (
    [(O, L, 0), (O, R, 1), (L, O, 0), (R, O, 1), (O, L, 1), (O, R, 0), (L, O, 1), (R, O, 0), (O, F, 0), (O, F, 1)]
    + [(F, O, 0), (F, O, 1)]
    + [(L, L, 0), (R, R, 1), (L, R, 1), (R, L, 0), (L, L, 1), (R, R, 0), (L, R, 0), (R, L, 1)]
    + [(F, L, 0), (F, R, 1), (L, F, 0), (R, F, 1), (L, F, 1), (R, F, 0)]
    + [(F, R, 0), (F, L, 1), (F, F, 0), (F, F, 1)]
)


def lookup(t, values):
    return sum((t == k).astype(jnp.int32) * v for k, v in enumerate(values) if v)


def fused(
    h_hbm, gain_ref, wq_hbm, wkv_hbm, pos_ref, freq_ref, order_ref,
    q_ref, kv_ref,
    rows, wq, wkv, w, part, inbox, kvs, cosines, sines,
    load_sem, a_send, a_recv, a_side_send, a_side_recv,
    k_send, k_recv, k_side_send, k_side_recv, r_send, r_recv,
):
    gx, gy, gz = lax.axis_index("gx"), lax.axis_index("gy"), lax.axis_index("gz")
    x, core, zh = gx // 2, gx % 2, gy
    zl, y = gz // 4, gz % 4
    tok = rows.shape[2]
    kdim = rows.shape[3]
    n_q = wq.shape[1]
    n_kv = wkv.shape[1]
    n_all = w.shape[1]

    def at(xx, cc, zz, yy, ll):
        return (2 * xx + cc, zz, ll * 4 + yy)

    sibling = at(x, 1 - core, zh, y, zl)
    x_up = at((x + 1) % 4, core, zh, y, zl)
    x_down = at((x + 3) % 4, core, zh, y, zl)
    z_up = at(x, core, (zh + 1) % 4, y, zl)
    z_down = at(x, core, (zh + 3) % 4, y, zl)

    loads = [
        pltpu.make_async_copy(h_hbm, rows.at[gx, gy], load_sem.at[0]),
        pltpu.make_async_copy(wq_hbm, wq, load_sem.at[1]),
        pltpu.make_async_copy(wkv_hbm, wkv, load_sem.at[2]),
    ]
    for load in loads:
        load.start()

    barrier = pltpu.get_barrier_semaphore()
    peers = [
        sibling, x_up, x_down, z_up, z_down,
        at(x, core, zh, (y + 1) % 4, zl), at(x, core, zh, (y + 3) % 4, zl), at(x, core, zh, y, 1 - zl),
    ]
    for peer in peers:
        pl.semaphore_signal(barrier, inc=1, device_id=peer, device_id_type=MESH)

    class Gather:
        def __init__(self, buf, send, recv, side_send, side_recv):
            self.buf, self.send, self.recv = buf, send, recv
            self.side_send, self.side_recv = side_send, side_recv
            self.size = buf.shape[2] // 2
            self.sent = []

        def piece(self, ox, oz, p, cls=None):
            c = core if cls is None else cls
            return self.buf.at[2 * ((x + ox) % 4) + c, (zh + oz) % 4, pl.ds(p * self.size, self.size)]

        def copy(self, which, index, recv_at, target):
            ref = self.piece(*which)
            return pltpu.make_async_remote_copy(
                src_ref=ref, dst_ref=ref, send_sem=self.send.at[index], recv_sem=self.recv.at[recv_at],
                device_id=target, device_id_type=MESH,
            )

        def push(self, ox, oz, p, to_x, to_z, target):
            args = (ox, oz, p), len(self.sent), (to_x, to_z, p), target
            self.copy(*args).start()
            self.sent.append(args)

        def side(self, ox, oz, p, cls=None):
            ref = self.piece(ox, oz, p, cls)
            return pltpu.make_async_remote_copy(
                src_ref=ref, dst_ref=ref, send_sem=self.side_send.at[ox, oz, p],
                recv_sem=self.side_recv.at[ox, oz, p], device_id=sibling, device_id_type=MESH,
            )

        def spread_x(self, oz, p):
            self.push(O, oz, p, L, oz, x_up)
            self.push(O, oz, p, R, oz, x_down)

        def begin(self):
            for p in (0, 1):
                self.push(O, O, p, O, L, z_up)
                self.push(O, O, 1 - p, O, R, z_down)
                self.push(O, O, p, L, O, x_up)
                self.push(O, O, 1 - p, R, O, x_down)
            for p in (0, 1):
                self.side(O, O, p).start()

        def arrive(self, ox, oz, p):
            self.copy((ox, oz, p), 0, (ox, oz, p), x_up).wait_recv()
            if ox == O:
                if (oz, p) == (L, 0):
                    self.push(O, L, 0, O, F, z_up)
                if (oz, p) == (R, 1):
                    self.push(O, R, 1, O, F, z_down)
                self.spread_x(oz, p)
            if (ox, p) == (L, 0):
                self.push(L, oz, 0, F, oz, x_up)
            if (ox, p) == (R, 1):
                self.push(R, oz, 1, F, oz, x_down)
            self.side(ox, oz, p).start()

        def finish(self):
            for args in self.sent:
                self.copy(*args).wait_send()
            for ox in range(4):
                for oz in range(4):
                    for p in (0, 1):
                        self.side(ox, oz, p).wait_send()

    gather = Gather(rows, a_send, a_recv, a_side_send, a_side_recv)
    kv_gather = Gather(kvs, k_send, k_recv, k_side_send, k_side_recv)

    loads[0].wait()
    pl.semaphore_wait(barrier, len(peers))
    gather.begin()

    loads[1].wait()
    loads[2].wait()
    side_len = 128
    row_id = lax.broadcasted_iota(jnp.int32, (side_len, side_len), 0)
    lane = lax.broadcasted_iota(jnp.int32, (side_len, side_len), 1)

    def scale(i, carry):
        diagonal = jnp.where(row_id == lane, jnp.broadcast_to(gain_ref[pl.ds(i, 1), :], (side_len, side_len)), 0.0)
        diagonal = diagonal.astype(BF16)
        band = pl.ds(pl.multiple_of(i * side_len, side_len), side_len)
        w[band, 0:n_q] = jnp.dot(diagonal, wq[band, :], preferred_element_type=F32).astype(BF16)
        narrow = jnp.dot(diagonal, wkv[band, :], preferred_element_type=F32)
        w[band, n_q:n_all] = jnp.concatenate([narrow, jnp.zeros((side_len, n_all - n_q - n_kv), F32)], axis=1).astype(BF16)
        return carry

    lax.fori_loop(0, kdim // side_len, scale, 0)

    def tables(i, carry):
        spread = jnp.broadcast_to(pos_ref[pl.ds(i, 1), :].astype(F32), (side_len, side_len))
        angles = jnp.transpose(spread) * freq_ref[0:1, :]
        band = pl.ds(pl.multiple_of(i * side_len, side_len), side_len)
        cosines[band, :] = jnp.cos(angles)
        s = jnp.sin(angles)
        sines[band, :] = jnp.where(lane % 2 == 0, -s, s)
        return carry

    lax.fori_loop(0, pos_ref.shape[0], tables, 0)
    kvs[gx, gy] = jnp.zeros(kvs.shape[2:], BF16)

    def unit(t, c):
        xx = (x + lookup(t, [s[0][0] for s in STEPS])) % 4
        zz = (zh + lookup(t, [s[0][1] for s in STEPS])) % 4
        y_own = (2 * xx + c) % 4
        zl_own = xx // 2
        step = 1 if c else 3
        relay, far, direct = (y_own + step) % 4, (y_own + 2) % 4, (y_own + 4 - step) % 4
        return xx, zz, y_own, zl_own, relay, far, direct

    def reduce_copy(t, c, slot, target):
        return pltpu.make_async_remote_copy(
            src_ref=part.at[t, c], dst_ref=inbox.at[t, c, slot], send_sem=r_send.at[t, c],
            recv_sem=r_recv.at[t, c, slot], device_id=target, device_id_type=MESH,
        )

    def landed(t, c, slot):
        reduce_copy(t, c, slot, sibling).wait_recv()

    tile_lane = lax.broadcasted_iota(jnp.int32, (tok, 128), 1)

    def split_square(tile):
        rest = tile - tile.astype(BF16).astype(F32)
        return jnp.where(tile_lane == n_kv + 1, tile + pltpu.roll(rest, 1, 1), tile).astype(BF16)

    def add_up(t, c, slots):
        for n0 in range(0, n_q, 128):
            cols = pl.ds(n0, 128)
            total = part[t, c, :, cols].astype(F32)
            for slot in slots:
                total = total + inbox[t, c, slot, :, cols].astype(F32)
            part[t, c, :, cols] = total.astype(BF16)
        cols = pl.ds(n_q, 128)
        total = part[t, c, :, cols].astype(F32)
        for slot in slots:
            total = total + inbox[t, c, slot, :, cols].astype(F32)
        part[t, c, :, cols] = split_square(total)

    def compute(t):
        xx, zz = unit(t, 0)[:2]
        ox = lookup(t, [s[0][0] for s in STEPS])
        oz = lookup(t, [s[0][1] for s in STEPS])
        for p in (0, 1):
            gather.side(ox, oz, p, 1 - core).wait_recv()
        pair = pl.ds(2 * xx, 2)
        squares = jnp.zeros((2 * tok, 128), F32)
        for k0 in range(0, kdim, 128):
            some = rows[pair, zz, :, k0 : k0 + 128].reshape(2 * tok, 128).astype(F32)
            squares = squares + some * some
        square = jnp.sum(squares, axis=1, keepdims=True)
        high = square.astype(BF16).astype(F32)
        low = square - high
        lhs = rows[pair, zz].reshape(2 * tok, kdim)
        for n0 in range(0, n_q, 256):
            c_tile = jnp.dot(lhs, w[:, n0 : n0 + 256], preferred_element_type=F32).astype(BF16)
            part[t, 0, :, n0 : n0 + 256] = c_tile[:tok]
            part[t, 1, :, n0 : n0 + 256] = c_tile[tok:]
        last = jnp.dot(lhs, w[:, n_q:n_all], preferred_element_type=F32)
        wide = lax.broadcasted_iota(jnp.int32, (2 * tok, 128), 1)
        last = jnp.where(wide == n_kv, high, jnp.where(wide == n_kv + 1, low, last)).astype(BF16)
        part[t, 0, :, n_q:n_all] = last[:tok]
        part[t, 1, :, n_q:n_all] = last[tok:]
        for c in (0, 1):
            _, _, y_own, _, relay, far, direct = unit(t, c)

            @pl.when(y == far)
            def _():
                reduce_copy(t, c, 0, at(x, core, zh, relay, zl)).start()

            @pl.when(y == direct)
            def _():
                reduce_copy(t, c, 0, at(x, core, zh, y_own, zl)).start()

    def relay_stage(t):
        for c in (0, 1):
            _, _, y_own, _, relay, far, direct = unit(t, c)

            @pl.when(y == relay)
            def _():
                landed(t, c, 0)
                add_up(t, c, [0])
                reduce_copy(t, c, 1, at(x, core, zh, y_own, zl)).start()

    def plane_stage(t):
        for c in (0, 1):
            _, _, y_own, zl_own, relay, far, direct = unit(t, c)

            @pl.when((y == y_own) & (zl != zl_own))
            def _():
                landed(t, c, 0)
                landed(t, c, 1)
                add_up(t, c, [0, 1])
                reduce_copy(t, c, 2, at(x, core, zh, y, zl_own)).start()

    def rotate(tile, cos_t, sin_t):
        swapped = jnp.where(tile_lane % 2 == 0, pltpu.roll(tile, 127, 1), pltpu.roll(tile, 1, 1))
        return tile * cos_t + swapped * sin_t

    def owner_stage(t):
        for c in (0, 1):
            _, zz, y_own, zl_own, relay, far, direct = unit(t, c)

            @pl.when((y == y_own) & (zl == zl_own))
            def _():
                for slot in range(3):
                    landed(t, c, slot)

                def total(n0):
                    cols = pl.ds(n0, 128)
                    value = part[t, c, :, cols].astype(F32)
                    for slot in range(3):
                        value = value + inbox[t, c, slot, :, cols].astype(F32)
                    return value

                tail = total(n_q)
                square = jnp.sum(jnp.where((tile_lane == n_kv) | (tile_lane == n_kv + 1), tail, 0.0), axis=1, keepdims=True)
                factor = lax.rsqrt(square / D + norm_eps)
                band = pl.ds(pl.multiple_of(zz * tok, tok), tok)
                cos_t, sin_t = cosines[band, :], sines[band, :]
                for n0 in range(0, n_q, 128):
                    q_ref[band, n0 : n0 + 128] = rotate(total(n0) * factor, cos_t, sin_t).astype(BF16)
                tail = tail * factor
                odd = jnp.full((tok, 128), gy % 2, jnp.int32) == 1
                is_key = jnp.full((tok, 128), gy // 2, jnp.int32) == 0
                cos_k = jnp.where(odd, pltpu.roll(cos_t, 64, 1), cos_t)
                sin_k = jnp.where(odd, pltpu.roll(sin_t, 64, 1), sin_t)
                value = jnp.where(is_key, rotate(tail, cos_k, sin_k), tail)
                upper = jnp.full((tok, 128), zz // 2, jnp.int32)
                value = jnp.where(upper == 1, pltpu.roll(value, 64, 1), value)
                half = pl.ds(pl.multiple_of((zz % 2) * tok, tok), tok)
                old = kvs[gx, gy, half, :].astype(F32)
                kvs[gx, gy, half, :] = jnp.where(tile_lane // 64 == upper, value, old).astype(BF16)

    def step(t, carry):
        for k, (_, events) in enumerate(STEPS):
            if events:

                @pl.when(t == k)
                def _():
                    for event in events:
                        gather.arrive(*event)

        @pl.when(t < N_STEPS)
        def _():
            compute(t)

        @pl.when((t >= LAG_RELAY) & (t < N_STEPS + LAG_RELAY))
        def _():
            relay_stage(t - LAG_RELAY)

        @pl.when((t >= LAG_PLANE) & (t < N_STEPS + LAG_PLANE))
        def _():
            plane_stage(t - LAG_PLANE)

        @pl.when((t >= LAG_OWNER) & (t < N_STEPS + LAG_OWNER))
        def _():
            owner_stage(t - LAG_OWNER)

        return carry

    lax.fori_loop(0, N_STEPS + LAG_OWNER, step, 0)

    kv_gather.begin()
    for event in KV_EVENTS:
        kv_gather.arrive(*event)
    for ox in range(4):
        for oz in range(4):
            for p in (0, 1):
                kv_gather.side(ox, oz, p, 1 - core).wait_recv()
    slots = kv_ref.shape[0]
    half_rows = kvs.shape[2]
    half_lane = lax.broadcasted_iota(jnp.int32, (half_rows, 128), 1)
    for s in range(slots):
        head = order_ref[slots * gy + s]
        for g in (0, 1):
            first = kvs[head, 2 * g].astype(F32)
            second = kvs[head, 2 * g + 1].astype(F32)
            cols = slice(g * 128, g * 128 + 128)
            kv_ref[s, 0:half_rows, cols] = jnp.where(half_lane < 64, first, pltpu.roll(second, 64, 1)).astype(BF16)
            kv_ref[s, half_rows : 2 * half_rows, cols] = jnp.where(half_lane < 64, pltpu.roll(first, 64, 1), second).astype(BF16)

    gather.finish()
    kv_gather.finish()

    def drain(t, carry):
        for c in (0, 1):
            _, _, y_own, zl_own, relay, far, direct = unit(t, c)

            @pl.when((y != y_own) | (zl != zl_own))
            def _():
                reduce_copy(t, c, 0, sibling).wait_send()

        return carry

    lax.fori_loop(0, N_STEPS, drain, 0)


def body(hidden_rows, norm_gain, w_query, w_keyval, positions, keyval_order):
    tok, kdim = hidden_rows.shape
    n_q, n_kv = w_query.shape[1], w_keyval.shape[1]
    n_all = n_q + 128
    n_tok = positions.shape[0]
    freq = np.exp((np.arange(128) // 2) * (-2.0 * math.log(rope_base) / HD)).astype(np.float32)[None, :]
    hbm = pl.BlockSpec(memory_space=pl.ANY)
    vmem = pl.BlockSpec(memory_space=pltpu.VMEM)
    dma = pltpu.SemaphoreType.DMA
    return pl.pallas_call(
        fused,
        out_shape=(
            jax.ShapeDtypeStruct((n_tok, n_q), BF16),
            jax.ShapeDtypeStruct((2, n_tok, 2 * HD), BF16),
        ),
        in_specs=[hbm, vmem, hbm, hbm, vmem, vmem, pl.BlockSpec(memory_space=pltpu.SMEM)],
        out_specs=(vmem, vmem),
        scratch_shapes=[
            pltpu.VMEM((8, 4, tok, kdim), BF16),
            pltpu.VMEM((kdim, n_q), BF16),
            pltpu.VMEM((kdim, n_kv), BF16),
            pltpu.VMEM((kdim, n_all), BF16),
            pltpu.VMEM((N_STEPS, 2, tok, n_all), BF16),
            pltpu.VMEM((N_STEPS, 2, 3, tok, n_all), BF16),
            pltpu.VMEM((8, 4, n_tok // 2, 128), BF16),
            pltpu.VMEM((n_tok, 128), F32),
            pltpu.VMEM((n_tok, 128), F32),
            dma((3,)),
            dma((30,)), dma((4, 4, 2)), dma((4, 4, 2)), dma((4, 4, 2)),
            dma((30,)), dma((4, 4, 2)), dma((4, 4, 2)), dma((4, 4, 2)),
            dma((N_STEPS, 2)), dma((N_STEPS, 2, 3)),
        ],
        compiler_params=pltpu.CompilerParams(
            collective_id=0, has_side_effects=True, vmem_limit_bytes=62 * 1024 * 1024
        ),
        name="fused",
    )(
        hidden_rows,
        norm_gain.astype(F32).reshape(-1, 128),
        w_query,
        w_keyval,
        positions.reshape(-1, 128),
        jnp.asarray(freq),
        keyval_order,
    )


def solution(mesh):
    in_specs = (
        P(("gx", "gy"), "gz"),
        P("gz"),
        P("gz", ("gx", "gy")),
        P("gz", ("gx", "gy")),
        P("gz"),
        P(),
    )
    out_specs = (P("gz", ("gx", "gy")), P("gy", "gz", None))
    return jax.shard_map(body, mesh=mesh, in_specs=in_specs, out_specs=out_specs, check_vma=False)
```

time: 269 us -> 135 us (0.50)
  waiting for transfers between devices: 169 us -> 0 us
  Pallas kernels: 0 us -> 127 us
  starting transfers between devices: 30.7 us -> 0 us
  matrix products: 27 us -> 0 us
  between operations: 14.2 us -> 0.64 us
  local copies, waits for them, and re-layouts: 16.5 us -> 5.69 us
  other arithmetic: 10.6 us -> 1.29 us
    all_gather x2 -> x0, waiting for transfers between devices: 165 us -> none  [the longest x1 107 us: body(): gathered = lax.all_gather(normed_rows, ('gx', 'gy'), axis=0, tiled=True)]
    pallas_call x0 -> x1, Pallas kernels: none -> 127 us  [body(): pl.pallas_call(fused, out_shape=(jax.ShapeDtypeStruct((n_tok, n_q), BF16)...]
    all_to_all x3 -> x0, starting transfers between devices: 30.5 us -> none  [the longest x2 24.1 us: summed_on_arrival(): lax.all_to_all(in_blocks(value, dim, count), axis, 0, 0, tiled=True)]
    dot_general x3 -> x0, matrix products: 27 us -> none  [the longest x1 13.7 us: body(): jnp.dot(gathered, w_query, preferred_element_type=jnp.float32)]
    reshape x4 -> x0, local copies, waits for them, and re-layouts: 7.32 us -> none  [the longest x1 4.55 us: body(): keyval_heads = keyval_all.reshape(keyval_all.shape[0], KVH, 2 * HD)]
    reduce_sum x4 -> x0, other arithmetic: 4.35 us -> none  [the longest x2 2.95 us: summed_on_arrival(): return jnp.sum(blocks.astype(jnp.float32), axis=0)]
    all_to_all x3 -> x0, waiting for transfers between devices: 4.23 us -> none  [the longest x1 4.22 us: from_everyone(): return lax.all_to_all(copies, axis, split_axis=0, concat_axis=0, tiled=True)]
    convert_element_type x4 -> x0, other arithmetic: 3.43 us -> none  [the longest x1 2.03 us: body(): normed_rows = (hidden_rows.astype(jnp.float32) * factor[:, None] * widene...]
  transfers between devices with their start and end apart: 5 -> 0, of which waited for: 3 -> 0; matrix products, arithmetic and copies ran while one was open for 9% -> 0% of each run, Pallas kernels for 0% -> 0%
where the time goes in v1:
time: 135 us
  Pallas kernels  127 us (94%)
  local copies, waits for them, and re-layouts  5.69 us (4%)
    pallas_call x1, Pallas kernels, body(): pl.pallas_call(fused, out_shape=(jax.ShapeDtypeStruct((n_tok, n_q), BF16)...  127 us
    unnamed x3, local copies, waits for them, and re-layouts  5.69 us

profile of v1, /device:TPU:1, one launch (start us, length us, event | category | flops | bytes accessed | tf_op | source)
XLA Modules:
  0.0 134.9 jit_solution(6873575400842119427)
XLA Ops:
  0.6 1.3 bitcast_convert_fusion.gain_ref
  1.9 2.0 %copy.9.wkv_hbm = bf16[2048,64]{1,0:T(8,128)(2,1)} copy(bf16[2048,64]{0,1:T(8,128)(2,1)} %param.10) | data formatting | bytes 524288 | tf_op args[3]
  3.9 127.3 %fused.1 = (bf16[512,512]{1,0:T(8,128)(2,1)}, bf16[2,512,256]{2,1,0:T(8,128)(2,1)}) custom-call(bf16[128,2048]{1,0:T(8,128)(2,1)} %h_hbm.1, f32[16,128]{1,0:T(8,128)} %bitcast_convert_fusion.gain_ref, bf16[2048,512]{1,0:T(8,128)(2,1)} %wq_hbm.1, bf16[2048,64]{1,0:T(8,128)(2,1)} %copy.9.wkv_hbm, s32[4,128]{1,0:T(4,128)} %bitcast.4, ...), custom_call_target="tpu_custom_call" | custom-call | tf_op jit(solution)/shard_map/fused/pallas_call | solution.py:405
  131.2 1.9 %copy.12 = bf16[512,512]{1,0:T(8,128)(2,1)} copy(bf16[512,512]{1,0:T(8,128)(2,1)} %get-tuple-element.4) | data formatting | bytes 1048576
  133.0 1.9 %copy.13 = bf16[2,512,256]{2,1,0:T(8,128)(2,1)} copy(bf16[2,512,256]{2,1,0:T(8,128)(2,1)} %get-tuple-element.5) | data formatting | bytes 1048576

commit v2 on v1

--- a/solution.py
+++ b/solution.py
@@ -58,9 +58,9 @@
 def fused(
     h_hbm, gain_ref, wq_hbm, wkv_hbm, pos_ref, freq_ref, order_ref,
     q_ref, kv_ref,
-    rows, wq, wkv, w, part, inbox, kvs, cosines, sines,
+    rows, wq, wkv, w, part, part_kv, inbox, inbox_kv, kvs, factors, cosines, sines,
     load_sem, a_send, a_recv, a_side_send, a_side_recv,
-    k_send, k_recv, k_side_send, k_side_recv, r_send, r_recv,
+    k_send, k_recv, k_side_send, k_side_recv, r_send, r_recv, r_kv_send, r_kv_recv,
 ):
     gx, gy, gz = lax.axis_index("gx"), lax.axis_index("gy"), lax.axis_index("gz")
     x, core, zh = gx // 2, gx % 2, gy
@@ -68,7 +68,7 @@
     tok = rows.shape[2]
     kdim = rows.shape[3]
     n_q = wq.shape[1]
-    n_kv = wkv.shape[1]
+    n_kv = wkv.shape[0]
     n_all = w.shape[1]
 
     def at(xx, cc, zz, yy, ll):
@@ -174,16 +174,13 @@
     row_id = lax.broadcasted_iota(jnp.int32, (side_len, side_len), 0)
     lane = lax.broadcasted_iota(jnp.int32, (side_len, side_len), 1)
 
-    def scale(i, carry):
-        diagonal = jnp.where(row_id == lane, jnp.broadcast_to(gain_ref[pl.ds(i, 1), :], (side_len, side_len)), 0.0)
-        diagonal = diagonal.astype(BF16)
-        band = pl.ds(pl.multiple_of(i * side_len, side_len), side_len)
+    for i in range(kdim // side_len):
+        band = slice(i * side_len, (i + 1) * side_len)
+        gain = jnp.broadcast_to(gain_ref[:, band].astype(F32), (side_len, side_len))
+        diagonal = jnp.where(row_id == lane, gain, 0.0).astype(BF16)
         w[band, 0:n_q] = jnp.dot(diagonal, wq[band, :], preferred_element_type=F32).astype(BF16)
-        narrow = jnp.dot(diagonal, wkv[band, :], preferred_element_type=F32)
+        narrow = lax.dot_general(diagonal, wkv[:, band], (((1,), (1,)), ((), ())), preferred_element_type=F32)
         w[band, n_q:n_all] = jnp.concatenate([narrow, jnp.zeros((side_len, n_all - n_q - n_kv), F32)], axis=1).astype(BF16)
-        return carry
-
-    lax.fori_loop(0, kdim // side_len, scale, 0)
 
     def tables(i, carry):
         spread = jnp.broadcast_to(pos_ref[pl.ds(i, 1), :].astype(F32), (side_len, side_len))
@@ -206,33 +203,125 @@
         relay, far, direct = (y_own + step) % 4, (y_own + 2) % 4, (y_own + 4 - step) % 4
         return xx, zz, y_own, zl_own, relay, far, direct
 
-    def reduce_copy(t, c, slot, target):
-        return pltpu.make_async_remote_copy(
-            src_ref=part.at[t, c], dst_ref=inbox.at[t, c, slot], send_sem=r_send.at[t, c],
-            recv_sem=r_recv.at[t, c, slot], device_id=target, device_id_type=MESH,
-        )
-
-    def landed(t, c, slot):
-        reduce_copy(t, c, slot, sibling).wait_recv()
+    class Reduction:
+        def __init__(self, part, inbox, send, recv):
+            self.part, self.inbox, self.send, self.recv = part, inbox, send, recv
+
+        def copy(self, t, c, slot, target):
+            return pltpu.make_async_remote_copy(
+                src_ref=self.part.at[t, c], dst_ref=self.inbox.at[t, c, slot], send_sem=self.send.at[t, c],
+                recv_sem=self.recv.at[t, c, slot], device_id=target, device_id_type=MESH,
+            )
+
+        def landed(self, t, c, slot):
+            self.copy(t, c, slot, sibling).wait_recv()
+
+        def total(self, t, c, slots, cols):
+            value = self.part[t, c, :, cols].astype(F32)
+            for slot in slots:
+                value = value + self.inbox[t, c, slot, :, cols].astype(F32)
+            return value
+
+        def first(self, t):
+            for c in (0, 1):
+                _, _, y_own, _, relay, far, direct = unit(t, c)
+
+                @pl.when(y == far)
+                def _():
+                    self.copy(t, c, 0, at(x, core, zh, relay, zl)).start()
+
+                @pl.when(y == direct)
+                def _():
+                    self.copy(t, c, 0, at(x, core, zh, y_own, zl)).start()
+
+        def relay(self, t):
+            for c in (0, 1):
+                _, _, y_own, _, relay, far, direct = unit(t, c)
+
+                @pl.when(y == relay)
+                def _():
+                    self.landed(t, c, 0)
+                    self.add_up(t, c, [0])
+                    self.copy(t, c, 1, at(x, core, zh, y_own, zl)).start()
+
+        def plane(self, t):
+            for c in (0, 1):
+                _, _, y_own, zl_own, relay, far, direct = unit(t, c)
+
+                @pl.when((y == y_own) & (zl != zl_own))
+                def _():
+                    self.landed(t, c, 0)
+                    self.landed(t, c, 1)
+                    self.add_up(t, c, [0, 1])
+                    self.copy(t, c, 2, at(x, core, zh, y, zl_own)).start()
+
+        def owner(self, t):
+            for c in (0, 1):
+                _, zz, y_own, zl_own, relay, far, direct = unit(t, c)
+
+                @pl.when((y == y_own) & (zl == zl_own))
+                def _():
+                    for slot in range(3):
+                        self.landed(t, c, slot)
+                    self.store(t, c, zz)
+
+        def drain(self, t):
+            for c in (0, 1):
+                _, _, y_own, zl_own, relay, far, direct = unit(t, c)
+
+                @pl.when((y != y_own) | (zl != zl_own))
+                def _():
+                    self.copy(t, c, 0, sibling).wait_send()
 
     tile_lane = lax.broadcasted_iota(jnp.int32, (tok, 128), 1)
 
-    def split_square(tile):
-        rest = tile - tile.astype(BF16).astype(F32)
-        return jnp.where(tile_lane == n_kv + 1, tile + pltpu.roll(rest, 1, 1), tile).astype(BF16)
-
-    def add_up(t, c, slots):
-        for n0 in range(0, n_q, 128):
-            cols = pl.ds(n0, 128)
-            total = part[t, c, :, cols].astype(F32)
-            for slot in slots:
-                total = total + inbox[t, c, slot, :, cols].astype(F32)
-            part[t, c, :, cols] = total.astype(BF16)
-        cols = pl.ds(n_q, 128)
-        total = part[t, c, :, cols].astype(F32)
-        for slot in slots:
-            total = total + inbox[t, c, slot, :, cols].astype(F32)
-        part[t, c, :, cols] = split_square(total)
+    def rotate(tile, cos_t, sin_t):
+        swapped = jnp.where(tile_lane % 2 == 0, pltpu.roll(tile, 127, 1), pltpu.roll(tile, 1, 1))
+        return tile * cos_t + swapped * sin_t
+
+    class QueryReduction(Reduction):
+        def add_up(self, t, c, slots):
+            for n0 in range(0, n_q, 128):
+                cols = slice(n0, n0 + 128)
+                self.part[t, c, :, cols] = self.total(t, c, slots, cols).astype(BF16)
+
+        def store(self, t, c, zz):
+            band = pl.ds(pl.multiple_of(zz * tok, tok), tok)
+            factor, cos_t, sin_t = factors[band, :], cosines[band, :], sines[band, :]
+            for n0 in range(0, n_q, 128):
+                cols = slice(n0, n0 + 128)
+                value = self.total(t, c, range(3), cols) * factor
+                q_ref[band, cols] = rotate(value, cos_t, sin_t).astype(BF16)
+
+    class KeyValueReduction(Reduction):
+        def add_up(self, t, c, slots):
+            tile = self.total(t, c, slots, slice(0, 128))
+            rest = tile - tile.astype(BF16).astype(F32)
+            tile = jnp.where(tile_lane == n_kv + 1, tile + pltpu.roll(rest, 1, 1), tile)
+            self.part[t, c] = tile.astype(BF16)
+
+        def store(self, t, c, zz):
+            band = pl.ds(pl.multiple_of(zz * tok, tok), tok)
+            tile = self.total(t, c, range(3), slice(0, 128))
+            is_square = (tile_lane == n_kv) | (tile_lane == n_kv + 1)
+            square = jnp.sum(jnp.where(is_square, tile, 0.0), axis=1, keepdims=True)
+            factor = jnp.broadcast_to(lax.rsqrt(square / D + norm_eps), (tok, 128))
+            factors[band, :] = factor
+            tile = tile * factor
+            cos_t, sin_t = cosines[band, :], sines[band, :]
+            odd = jnp.full((tok, 128), gy % 2, jnp.int32) == 1
+            is_key = jnp.full((tok, 128), gy // 2, jnp.int32) == 0
+            cos_t = jnp.where(odd, pltpu.roll(cos_t, 64, 1), cos_t)
+            sin_t = jnp.where(odd, pltpu.roll(sin_t, 64, 1), sin_t)
+            tile = jnp.where(is_key, rotate(tile, cos_t, sin_t), tile)
+            upper = jnp.full((tok, 128), zz // 2, jnp.int32)
+            tile = jnp.where(upper == 1, pltpu.roll(tile, 64, 1), tile)
+            half = pl.ds(pl.multiple_of((zz % 2) * tok, tok), tok)
+            old = kvs[gx, gy, half, :].astype(F32)
+            kvs[gx, gy, half, :] = jnp.where(tile_lane // 64 == upper, tile, old).astype(BF16)
+
+    query = QueryReduction(part, inbox, r_send, r_recv)
+    keyval = KeyValueReduction(part_kv, inbox_kv, r_kv_send, r_kv_recv)
 
     def compute(t):
         xx, zz = unit(t, 0)[:2]
@@ -249,85 +338,17 @@
         high = square.astype(BF16).astype(F32)
         low = square - high
         lhs = rows[pair, zz].reshape(2 * tok, kdim)
+        last = jnp.dot(lhs, w[:, n_q:n_all], preferred_element_type=F32)
+        wide = lax.broadcasted_iota(jnp.int32, (2 * tok, 128), 1)
+        last = jnp.where(wide == n_kv, high, jnp.where(wide == n_kv + 1, low, last)).astype(BF16)
+        part_kv[t, 0] = last[:tok]
+        part_kv[t, 1] = last[tok:]
+        keyval.first(t)
         for n0 in range(0, n_q, 256):
             c_tile = jnp.dot(lhs, w[:, n0 : n0 + 256], preferred_element_type=F32).astype(BF16)
             part[t, 0, :, n0 : n0 + 256] = c_tile[:tok]
             part[t, 1, :, n0 : n0 + 256] = c_tile[tok:]
-        last = jnp.dot(lhs, w[:, n_q:n_all], preferred_element_type=F32)
-        wide = lax.broadcasted_iota(jnp.int32, (2 * tok, 128), 1)
-        last = jnp.where(wide == n_kv, high, jnp.where(wide == n_kv + 1, low, last)).astype(BF16)
-        part[t, 0, :, n_q:n_all] = last[:tok]
-        part[t, 1, :, n_q:n_all] = last[tok:]
-        for c in (0, 1):
-            _, _, y_own, _, relay, far, direct = unit(t, c)
-
-            @pl.when(y == far)
-            def _():
-                reduce_copy(t, c, 0, at(x, core, zh, relay, zl)).start()
-
-            @pl.when(y == direct)
-            def _():
-                reduce_copy(t, c, 0, at(x, core, zh, y_own, zl)).start()
-
-    def relay_stage(t):
-        for c in (0, 1):
-            _, _, y_own, _, relay, far, direct = unit(t, c)
-
-            @pl.when(y == relay)
-            def _():
-                landed(t, c, 0)
-                add_up(t, c, [0])
-                reduce_copy(t, c, 1, at(x, core, zh, y_own, zl)).start()
-
-    def plane_stage(t):
-        for c in (0, 1):
-            _, _, y_own, zl_own, relay, far, direct = unit(t, c)
-
-            @pl.when((y == y_own) & (zl != zl_own))
-            def _():
-                landed(t, c, 0)
-                landed(t, c, 1)
-                add_up(t, c, [0, 1])
-                reduce_copy(t, c, 2, at(x, core, zh, y, zl_own)).start()
-
-    def rotate(tile, cos_t, sin_t):
-        swapped = jnp.where(tile_lane % 2 == 0, pltpu.roll(tile, 127, 1), pltpu.roll(tile, 1, 1))
-        return tile * cos_t + swapped * sin_t
-
-    def owner_stage(t):
-        for c in (0, 1):
-            _, zz, y_own, zl_own, relay, far, direct = unit(t, c)
-
-            @pl.when((y == y_own) & (zl == zl_own))
-            def _():
-                for slot in range(3):
-                    landed(t, c, slot)
-
-                def total(n0):
-                    cols = pl.ds(n0, 128)
-                    value = part[t, c, :, cols].astype(F32)
-                    for slot in range(3):
-                        value = value + inbox[t, c, slot, :, cols].astype(F32)
-                    return value
-
-                tail = total(n_q)
-                square = jnp.sum(jnp.where((tile_lane == n_kv) | (tile_lane == n_kv + 1), tail, 0.0), axis=1, keepdims=True)
-                factor = lax.rsqrt(square / D + norm_eps)
-                band = pl.ds(pl.multiple_of(zz * tok, tok), tok)
-                cos_t, sin_t = cosines[band, :], sines[band, :]
-                for n0 in range(0, n_q, 128):
-                    q_ref[band, n0 : n0 + 128] = rotate(total(n0) * factor, cos_t, sin_t).astype(BF16)
-                tail = tail * factor
-                odd = jnp.full((tok, 128), gy % 2, jnp.int32) == 1
-                is_key = jnp.full((tok, 128), gy // 2, jnp.int32) == 0
-                cos_k = jnp.where(odd, pltpu.roll(cos_t, 64, 1), cos_t)
-                sin_k = jnp.where(odd, pltpu.roll(sin_t, 64, 1), sin_t)
-                value = jnp.where(is_key, rotate(tail, cos_k, sin_k), tail)
-                upper = jnp.full((tok, 128), zz // 2, jnp.int32)
-                value = jnp.where(upper == 1, pltpu.roll(value, 64, 1), value)
-                half = pl.ds(pl.multiple_of((zz % 2) * tok, tok), tok)
-                old = kvs[gx, gy, half, :].astype(F32)
-                kvs[gx, gy, half, :] = jnp.where(tile_lane // 64 == upper, value, old).astype(BF16)
+        query.first(t)
 
     def step(t, carry):
         for k, (_, events) in enumerate(STEPS):
@@ -338,29 +359,38 @@
                     for event in events:
                         gather.arrive(*event)
 
-        @pl.when(t < N_STEPS)
-        def _():
-            compute(t)
-
-        @pl.when((t >= LAG_RELAY) & (t < N_STEPS + LAG_RELAY))
-        def _():
-            relay_stage(t - LAG_RELAY)
-
-        @pl.when((t >= LAG_PLANE) & (t < N_STEPS + LAG_PLANE))
-        def _():
-            plane_stage(t - LAG_PLANE)
-
-        @pl.when((t >= LAG_OWNER) & (t < N_STEPS + LAG_OWNER))
-        def _():
-            owner_stage(t - LAG_OWNER)
+        compute(t)
+        for lag, stage in (
+            (LAG_RELAY, "relay"), (LAG_PLANE, "plane"), (LAG_OWNER, "owner"),
+        ):
+
+            @pl.when(t >= lag)
+            def _():
+                getattr(keyval, stage)(t - lag)
+                getattr(query, stage)(t - lag)
 
         return carry
 
-    lax.fori_loop(0, N_STEPS + LAG_OWNER, step, 0)
-
+    lax.fori_loop(0, N_STEPS, step, 0)
+
+    def stages(stage, begin, end=N_STEPS):
+        lax.fori_loop(begin, end, lambda t, carry: (stage(t), carry)[1], 0)
+
+    stages(keyval.relay, N_STEPS - LAG_RELAY)
+    stages(query.relay, N_STEPS - LAG_RELAY)
+    stages(keyval.plane, N_STEPS - LAG_PLANE)
+    stages(keyval.owner, N_STEPS - LAG_OWNER)
     kv_gather.begin()
-    for event in KV_EVENTS:
+    stages(query.plane, N_STEPS - LAG_PLANE, N_STEPS - 2)
+    for event in KV_EVENTS[:8]:
         kv_gather.arrive(*event)
+    stages(query.plane, N_STEPS - 2)
+    for event in KV_EVENTS[8:20]:
+        kv_gather.arrive(*event)
+    stages(query.owner, N_STEPS - LAG_OWNER, N_STEPS - 2)
+    for event in KV_EVENTS[20:]:
+        kv_gather.arrive(*event)
+    stages(query.owner, N_STEPS - 2)
     for ox in range(4):
         for oz in range(4):
             for p in (0, 1):
@@ -380,17 +410,25 @@
     gather.finish()
     kv_gather.finish()
 
-    def drain(t, carry):
-        for c in (0, 1):
-            _, _, y_own, zl_own, relay, far, direct = unit(t, c)
-
-            @pl.when((y != y_own) | (zl != zl_own))
-            def _():
-                reduce_copy(t, c, 0, sibling).wait_send()
-
-        return carry
-
-    lax.fori_loop(0, N_STEPS, drain, 0)
+    stages(keyval.drain, 0)
+    stages(query.drain, 0)
+
+
+def pass_on(q_in, kv_in, q_out, kv_out, q_buf, kv_buf, sems):
+    takes, puts = [], []
+    for n, (source, buf, target) in enumerate(((q_in, q_buf, q_out), (kv_in, kv_buf, kv_out))):
+        half = buf.shape[0] // 2
+        for i in (0, 1):
+            piece = pl.ds(i * half, half)
+            takes.append(pltpu.make_async_copy(source.at[piece], buf.at[piece], sems.at[0, n, i]))
+            puts.append(pltpu.make_async_copy(buf.at[piece], target.at[piece], sems.at[1, n, i]))
+    for take in takes:
+        take.start()
+    for take, put in zip(takes, puts):
+        take.wait()
+        put.start()
+    for put in puts:
+        put.wait()
 
 
 def body(hidden_rows, norm_gain, w_query, w_keyval, positions, keyval_order):
@@ -402,27 +440,32 @@
     hbm = pl.BlockSpec(memory_space=pl.ANY)
     vmem = pl.BlockSpec(memory_space=pltpu.VMEM)
     dma = pltpu.SemaphoreType.DMA
-    return pl.pallas_call(
+    outs = (
+        jax.ShapeDtypeStruct((n_tok, n_q), BF16),
+        jax.ShapeDtypeStruct((2, n_tok, 2 * HD), BF16),
+    )
+    results = pl.pallas_call(
         fused,
-        out_shape=(
-            jax.ShapeDtypeStruct((n_tok, n_q), BF16),
-            jax.ShapeDtypeStruct((2, n_tok, 2 * HD), BF16),
-        ),
+        out_shape=outs,
         in_specs=[hbm, vmem, hbm, hbm, vmem, vmem, pl.BlockSpec(memory_space=pltpu.SMEM)],
         out_specs=(vmem, vmem),
         scratch_shapes=[
             pltpu.VMEM((8, 4, tok, kdim), BF16),
             pltpu.VMEM((kdim, n_q), BF16),
-            pltpu.VMEM((kdim, n_kv), BF16),
+            pltpu.VMEM((n_kv, kdim), BF16),
             pltpu.VMEM((kdim, n_all), BF16),
-            pltpu.VMEM((N_STEPS, 2, tok, n_all), BF16),
-            pltpu.VMEM((N_STEPS, 2, 3, tok, n_all), BF16),
+            pltpu.VMEM((N_STEPS, 2, tok, n_q), BF16),
+            pltpu.VMEM((N_STEPS, 2, tok, 128), BF16),
+            pltpu.VMEM((N_STEPS, 2, 3, tok, n_q), BF16),
+            pltpu.VMEM((N_STEPS, 2, 3, tok, 128), BF16),
             pltpu.VMEM((8, 4, n_tok // 2, 128), BF16),
+            pltpu.VMEM((n_tok, 128), F32),
             pltpu.VMEM((n_tok, 128), F32),
             pltpu.VMEM((n_tok, 128), F32),
             dma((3,)),
             dma((30,)), dma((4, 4, 2)), dma((4, 4, 2)), dma((4, 4, 2)),
             dma((30,)), dma((4, 4, 2)), dma((4, 4, 2)), dma((4, 4, 2)),
+            dma((N_STEPS, 2)), dma((N_STEPS, 2, 3)),
             dma((N_STEPS, 2)), dma((N_STEPS, 2, 3)),
         ],
         compiler_params=pltpu.CompilerParams(
@@ -431,13 +474,21 @@
         name="fused",
     )(
         hidden_rows,
-        norm_gain.astype(F32).reshape(-1, 128),
+        norm_gain.reshape(1, -1),
         w_query,
-        w_keyval,
+        w_keyval.T,
         positions.reshape(-1, 128),
         jnp.asarray(freq),
         keyval_order,
     )
+    return pl.pallas_call(
+        pass_on,
+        out_shape=outs,
+        in_specs=[hbm, hbm],
+        out_specs=(hbm, hbm),
+        scratch_shapes=[pltpu.VMEM(out.shape, out.dtype) for out in outs] + [dma((2, 2, 2))],
+        name="pass_on",
+    )(*results)
 
 
 def solution(mesh):

time: 135 us -> 125 us (0.926)
  Pallas kernels: 127 us -> 122 us
  local copies, waits for them, and re-layouts: 5.69 us -> 1.29 us
    unnamed x3 -> x0, local copies, waits for them, and re-layouts: 5.69 us -> none
    pallas_call x1 -> x2, Pallas kernels: 127 us -> 122 us  [the longest x1 120 us: body(): pl.pallas_call(fused, out_shape=outs, in_specs=[hbm, vmem, hbm, hbm, vmem...]
where the time goes in v2:
time: 125 us; the launch traced here: 124 us
  Pallas kernels  122 us (98%)
  local copies, waits for them, and re-layouts  1.29 us (1%)
    pallas_call x1, Pallas kernels, body(): pl.pallas_call(fused, out_shape=outs, in_specs=[hbm, vmem, hbm, hbm, vmem...  120 us

profile of v2, /device:TPU:1, one launch (start us, length us, event | category | flops | bytes accessed | tf_op | source)
XLA Modules:
  0.0 124.4 jit_solution(5866530888061104251)
XLA Ops:
  0.6 1.3 %reshape.10.gain_ref = bf16[1,2048]{1,0:T(2,128)(2,1)} reshape(bf16[2048]{0:T(1024)(128)(2,1)} %param.8) | data formatting | bytes 8192 | tf_op jit(solution)/shard_map/reshape | solution.py:477
  1.9 120.5 %fused.1 = (bf16[512,512]{1,0:T(8,128)(2,1)}, bf16[2,512,256]{2,1,0:T(8,128)(2,1)}) custom-call(bf16[128,2048]{1,0:T(8,128)(2,1)} %h_hbm.1, bf16[1,2048]{1,0:T(2,128)(2,1)} %reshape.10.gain_ref, bf16[2048,512]{1,0:T(8,128)(2,1)} %wq_hbm.1, bf16[64,2048]{1,0:T(8,128)(2,1)} %bitcast.2, s32[4,128]{1,0:T(4,128)} %bitcast.3, f32[1,128]{1,0:T(1,128)} %constant.2.clone.freq_ref, ...), custom_call_target="tpu_custom_call" | custom-call | tf_op jit(solution)/shard_map/fused/pallas_call | solution.py:447
  122.4 2.0 %pass_on.1 = (bf16[512,512]{1,0:T(8,128)(2,1)}, bf16[2,512,256]{2,1,0:T(8,128)(2,1)}) custom-call(bf16[512,512]{1,0:T(8,128)(2,1)} %get-tuple-element.4.q_in, bf16[2,512,256]{2,1,0:T(8,128)(2,1)} %get-tuple-element.5.kv_in), custom_call_target="tpu_custom_call" | custom-call | tf_op jit(solution)/shard_map/pass_on/pallas_call | solution.py:484

commit v3 on v2

v3 whole, which is shorter than its diff:
```python
import functools
import math

import jax
import jax.numpy as jnp
import numpy as np
from jax import lax
from jax.experimental import pallas as pl
from jax.experimental.pallas import tpu as pltpu
from jax.sharding import PartitionSpec as P

D = 16384
KVH = 8
HD = 128
rope_base = 500000.0
norm_eps = 1e-05

MESH = pl.DeviceIdType.MESH
F32 = jnp.float32
BF16 = jnp.bfloat16

O, L, R, F = 0, 3, 1, 2

ARRIVALS = [
    [],
    [(L, O, 0), (R, O, 1)],
    [(L, O, 1), (R, O, 0)],
    [(O, L, 0), (O, R, 1), "weights_own"],
    [(F, O, 0), (F, O, 1)],
    [(L, L, 0), (R, R, 1)],
    [(O, L, 1), (O, R, 0)],
    [(L, R, 1), (R, L, 0)],
    [(L, L, 1), (R, R, 0)],
    [(O, F, 0), (O, F, 1)],
    [(L, R, 0), (R, L, 1)],
    ["weights_near", (F, L, 0), (F, R, 1)],
    [(L, F, 0), (R, F, 1)],
    ["weights_far", "kv_products", (L, F, 1), (R, F, 0)],
    ["kv_relay", (F, R, 0), (F, L, 1)],
    ["kv_plane", (F, F, 0), (F, F, 1)],
]
STEPS = [(O, O, 0), (O, O, 1)] + [e for events in ARRIVALS for e in events if not isinstance(e, str)]
N_STEPS = len(STEPS)
PAIR = {step: n // 2 for n, step in enumerate(STEPS)}

SLOTS = [(events, 2 * n + 2, max(2 * n - 2, 0), max(2 * n - 6, 0)) for n, events in enumerate(ARRIVALS)] + [
    (["kv_owner"], 32, 32, 28),
    (["kv_near"], 32, 32, 32),
    (["kv_far"], 32, 32, 32),
]
KV_STEPS = (O, L, R, F)

KV_EVENTS = [
    [(O, L, 0), (O, R, 1)], [(L, O, 0), (R, O, 1)], [(O, L, 1), (O, R, 0)], [(L, O, 1), (R, O, 0)], [(O, F, 0), (O, F, 1)],
    [(F, O, 0), (F, O, 1)], [(L, L, 0), (R, R, 1)], [(L, R, 1), (R, L, 0)], [(L, L, 1), (R, R, 0)], [(L, R, 0), (R, L, 1)],
    [(F, L, 0), (F, R, 1)], [(L, F, 0), (R, F, 1)], [(L, F, 1), (R, F, 0)], [(F, R, 0), (F, L, 1)], [(F, F, 0), (F, F, 1)],
]


def lookup(t, values):
    return sum((t == k).astype(jnp.int32) * v for k, v in enumerate(values) if v)


def fused(
    h_hbm, gain_ref, wq_hbm, wkv_hbm, pos_ref, freq_ref, order_ref,
    q_hbm, kv_hbm,
    rows, wq, w, wkv, w_kv, part, part_kv, inbox, inbox_kv, kvs, factors, cosines, sines,
    load_sem, a_send, a_recv, a_side_send, a_side_recv,
    k_send, k_recv, k_side_send, k_side_recv, r_send, r_recv, r_kv_send, r_kv_recv,
    w_send, w_recv, q_ref, kv_ref, out_sem,
):
    gx, gy, gz = lax.axis_index("gx"), lax.axis_index("gy"), lax.axis_index("gz")
    x, core, zh = gx // 2, gx % 2, gy
    zl, y = gz // 4, gz % 4
    tok = rows.shape[2]
    part_tok = tok // 2
    kdim = rows.shape[3]
    n_q = wq.shape[1]
    n_kv = wkv.shape[1]
    n_head = 4 * n_kv

    def at(xx, cc, zz, yy, ll):
        return (2 * xx + cc, zz, ll * 4 + yy)

    sibling = at(x, 1 - core, zh, y, zl)
    x_up = at((x + 1) % 4, core, zh, y, zl)
    x_down = at((x + 3) % 4, core, zh, y, zl)
    z_up = at(x, core, (zh + 1) % 4, y, zl)
    z_down = at(x, core, (zh + 3) % 4, y, zl)

    loads = [
        pltpu.make_async_copy(h_hbm, rows.at[gx, gy], load_sem.at[0]),
        pltpu.make_async_copy(wq_hbm, wq, load_sem.at[1]),
        pltpu.make_async_copy(wkv_hbm, wkv.at[gy], load_sem.at[2]),
    ]
    for load in loads:
        load.start()

    barrier = pltpu.get_barrier_semaphore()
    peers = [
        sibling, x_up, x_down, z_up, z_down,
        at(x, core, zh, (y + 1) % 4, zl), at(x, core, zh, (y + 3) % 4, zl), at(x, core, zh, y, 1 - zl),
    ]
    for peer in peers:
        pl.semaphore_signal(barrier, inc=1, device_id=peer, device_id_type=MESH)

    class Gather:
        def __init__(self, buf, sends, recv, side_send, side_recv):
            self.buf, self.sends, self.recv = buf, sends, recv
            self.side_send, self.side_recv = side_send, side_recv
            self.size, self.extra = tok // 2, buf.shape[2] - tok

        def piece(self, ox, oz, p, whole=False):
            size = self.size + (self.extra if whole and p else 0)
            return self.buf.at[2 * ((x + ox) % 4) + core, (zh + oz) % 4, pl.ds(p * self.size, size)]

        def push(self, ox, oz, p, to_x, to_z, target):
            along_z = to_x == O
            ref = self.piece(ox, oz, p, whole=along_z)
            pltpu.make_async_remote_copy(
                src_ref=ref, dst_ref=ref, send_sem=self.sends.at[int(along_z)],
                recv_sem=self.recv.at[PAIR[to_x, to_z, p]], device_id=target, device_id_type=MESH,
            ).start()

        def side(self, ox, oz, p):
            ref = self.piece(ox, oz, p)
            n = PAIR[ox, oz, p] if self.side_recv.shape[0] > 1 else 0
            pltpu.make_async_remote_copy(
                src_ref=ref, dst_ref=ref, send_sem=self.side_send, recv_sem=self.side_recv.at[n],
                device_id=sibling, device_id_type=MESH,
            ).start()

        def begin(self):
            for p in (0, 1):
                self.push(O, O, p, O, L, z_up)
                self.push(O, O, 1 - p, O, R, z_down)
                self.push(O, O, p, L, O, x_up)
                self.push(O, O, 1 - p, R, O, x_down)
            for p in (0, 1):
                self.side(O, O, p)

        def arrive(self, *pieces):
            whole = self.buf.at[0, 0] if pieces[0][0] == O else self.buf.at[0, 0, pl.ds(0, tok)]
            received(whole, self.recv.at[PAIR[pieces[0]]])
            if (O, L, 0) in pieces:
                self.push(O, L, 0, O, F, z_up)
            if (O, R, 1) in pieces:
                self.push(O, R, 1, O, F, z_down)
            for ox, oz, p in pieces:
                if ox == O:
                    self.push(O, oz, p, L, oz, x_up)
                if (ox, p) == (L, 0):
                    self.push(L, oz, 0, F, oz, x_up)
            for ox, oz, p in pieces[::-1]:
                if ox == O:
                    self.push(O, oz, p, R, oz, x_down)
                if (ox, p) == (R, 1):
                    self.push(R, oz, 1, F, oz, x_down)
            for piece in pieces:
                self.side(*piece)

        def finish(self):
            left(self.buf.at[pl.ds(0, 8), pl.ds(0, 3), pl.ds(0, self.size)], self.sends.at[0])
            left(self.buf.at[0, pl.ds(0, 3)], self.sends.at[1])
            left(self.buf.at[:, :, pl.ds(0, self.size)], self.side_send)

    def received(ref, sem):
        pltpu.make_async_remote_copy(
            src_ref=ref, dst_ref=ref, send_sem=a_side_send, recv_sem=sem, device_id=sibling, device_id_type=MESH
        ).wait_recv()

    def left(ref, sem):
        pltpu.make_async_remote_copy(
            src_ref=ref, dst_ref=ref, send_sem=sem, recv_sem=a_recv.at[0], device_id=sibling, device_id_type=MESH
        ).wait_send()

    gather = Gather(rows, a_send, a_recv, a_side_send, a_side_recv)
    kv_gather = Gather(kvs, k_send, k_recv, k_side_send, k_side_recv)

    half_kv = n_kv // 2

    def weights_copy(oz, p, to_z, target):
        ref = wkv.at[(zh + oz) % 4, pl.ds(p * half_kv, half_kv)]
        return pltpu.make_async_remote_copy(
            src_ref=ref, dst_ref=ref, send_sem=w_send, recv_sem=w_recv.at[0 if (to_z, p) in ((L, 0), (R, 1)) else 1],
            device_id=target, device_id_type=MESH,
        )

    weights_sent = [
        (O, 0, L, z_up), (O, 1, R, z_down), (O, 1, L, z_up), (O, 0, R, z_down),
        (L, 0, F, z_up), (R, 1, F, z_down),
    ]

    def weights_own():
        for args in weights_sent[:4]:
            weights_copy(*args).start()

    def weights_near():
        received(wkv.at[0], w_recv.at[0])
        for args in weights_sent[4:]:
            weights_copy(*args).start()

    def weights_far():
        received(wkv.at[pl.ds(0, 2)], w_recv.at[1])
        for g in range(4):
            w_kv[g * n_kv : (g + 1) * n_kv, :] = (wkv[g].astype(F32) * gain_ref[...].astype(F32)).astype(BF16)

    loads[0].wait()
    loads[2].wait()
    pl.semaphore_wait(barrier, len(peers))
    gather.begin()

    loads[1].wait()
    side_len = 128
    row_id = lax.broadcasted_iota(jnp.int32, (side_len, side_len), 0)
    lane = lax.broadcasted_iota(jnp.int32, (side_len, side_len), 1)

    for i in range(kdim // side_len):
        band = slice(i * side_len, (i + 1) * side_len)
        gain = jnp.broadcast_to(gain_ref[:, band].astype(F32), (side_len, side_len))
        diagonal = jnp.where(row_id == lane, gain, 0.0).astype(BF16)
        w[band, 0:n_q] = jnp.dot(diagonal, wq[band, :], preferred_element_type=F32).astype(BF16)

    def tables(i, carry):
        spread = jnp.broadcast_to(pos_ref[pl.ds(i, 1), :].astype(F32), (side_len, side_len))
        angles = jnp.transpose(spread) * freq_ref[0:1, :]
        band = pl.ds(pl.multiple_of(i * side_len, side_len), side_len)
        cosines[band, :] = jnp.cos(angles)
        s = jnp.sin(angles)
        sines[band, :] = jnp.where(lane % 2 == 0, -s, s)
        return carry

    lax.fori_loop(0, pos_ref.shape[0], tables, 0)

    def unit(t, xx, c):
        y_own = (2 * xx + c) % 4
        zl_own = xx // 2
        step = 1 + 2 * ((t + c) % 2)
        relay, far, direct = (y_own + step) % 4, (y_own + 2) % 4, (y_own + 4 - step) % 4
        return y_own, zl_own, relay, far, direct

    class Reduction:
        def __init__(self, part, inbox, send, recv):
            self.part, self.inbox, self.send, self.recv = part, inbox, send, recv

        def copy(self, t, c, slot, target):
            return pltpu.make_async_remote_copy(
                src_ref=self.own(t, c), dst_ref=self.inbox.at[t, c, slot], send_sem=self.send,
                recv_sem=self.recv.at[t, c], device_id=target, device_id_type=MESH,
            )

        def landed(self, t, c, count):
            received(self.inbox.at[t, c, pl.ds(0, count)], self.recv.at[t, c])

        def total(self, t, c, slots, band, cols):
            value = self.own(t, c)[band, cols].astype(F32)
            for slot in slots:
                value = value + self.inbox[t, c, slot, band, cols].astype(F32)
            return value

        def first(self, t):
            for c in (0, 1):
                y_own, _, relay, far, direct = unit(t, self.place(t)[0], c)

                @pl.when(y == far)
                def _():
                    self.copy(t, c, 0, at(x, core, zh, relay, zl)).start()

                @pl.when(y == direct)
                def _():
                    self.copy(t, c, 0, at(x, core, zh, y_own, zl)).start()

        def relay(self, t):
            for c in (0, 1):
                y_own, _, relay, far, direct = unit(t, self.place(t)[0], c)

                @pl.when(y == relay)
                def _():
                    self.landed(t, c, 1)
                    self.add_up(t, c, [0])
                    self.copy(t, c, 1, at(x, core, zh, y_own, zl)).start()

        def plane(self, t):
            for c in (0, 1):
                y_own, zl_own, relay, far, direct = unit(t, self.place(t)[0], c)

                @pl.when((y == y_own) & (zl != zl_own))
                def _():
                    self.landed(t, c, 2)
                    self.add_up(t, c, [0, 1])
                    self.copy(t, c, 2, at(x, core, zh, y, zl_own)).start()

        def owner(self, t):
            for c in (0, 1):
                xx, zz = self.place(t)
                y_own, zl_own, relay, far, direct = unit(t, xx, c)

                @pl.when((y == y_own) & (zl == zl_own))
                def _():
                    self.landed(t, c, 3)
                    self.store(t, c, zz)

    tile_lane = lax.broadcasted_iota(jnp.int32, (tok, 128), 1)
    short_row = lax.broadcasted_iota(jnp.int32, (16, 128), 0)

    def rotate(tile, cos_t, sin_t):
        swapped = jnp.where(tile_lane[: tile.shape[0]] % 2 == 0, pltpu.roll(tile, 127, 1), pltpu.roll(tile, 1, 1))
        return tile * cos_t + swapped * sin_t

    class QueryReduction(Reduction):
        def place(self, t):
            return (x + lookup(t, [s[0] for s in STEPS])) % 4, (zh + lookup(t, [s[1] for s in STEPS])) % 4

        def own(self, t, c):
            return self.part.at[t, c]

        def rows_of(self, t):
            return lookup(t, [s[2] for s in STEPS]) * part_tok

        def add_up(self, t, c, slots):
            for n0 in range(0, n_q, 128):
                cols = slice(n0, n0 + 128)
                self.own(t, c)[:, cols] = self.total(t, c, slots, slice(None), cols).astype(BF16)

        def store(self, t, c, zz):
            band = pl.ds(pl.multiple_of(zz * tok + self.rows_of(t), part_tok), part_tok)
            cos_t, sin_t, factor = cosines[band, :], sines[band, :], factors[band, :]
            for n0 in range(0, n_q, 128):
                cols = slice(n0, n0 + 128)
                value = self.total(t, c, range(3), slice(None), cols) * factor
                q_ref[band, cols] = rotate(value, cos_t, sin_t).astype(BF16)

    class KeyValueReduction(Reduction):
        def place(self, k):
            return (x + lookup(k, KV_STEPS)) % 4, zh

        def own(self, k, c):
            return self.part.at[2 * k + c]

        def add_up(self, t, c, slots):
            tile = self.total(t, c, slots, pl.ds(tok, 16), slice(0, 128))
            rest = tile - tile.astype(BF16).astype(F32)
            tile = jnp.where(short_row == 1, tile + pltpu.roll(rest, 1, 0), tile)
            self.own(t, c)[tok : tok + 16, 0:128] = tile.astype(BF16)
            for n0 in range(0, n_head, 128):
                cols = slice(n0, n0 + 128)
                self.own(t, c)[0:tok, cols] = self.total(t, c, slots, pl.ds(0, tok), cols).astype(BF16)

        def store(self, t, c, zz):
            band = pl.ds(pl.multiple_of(zz * tok, tok), tok)
            tile = self.total(t, c, range(3), pl.ds(tok, 16), slice(0, 128))
            square = jnp.sum(jnp.where(short_row < 2, tile, 0.0), axis=0, keepdims=True)
            factor = lax.rsqrt(square / D + norm_eps)
            first = factor.astype(BF16).astype(F32)
            second = (factor - first).astype(BF16).astype(F32)
            third = factor - first - second
            spread = jnp.where(short_row == 0, first, jnp.where(short_row == 1, second, third))
            kvs[gx, gy, tok : tok + 16, 0:128] = spread.astype(BF16)
            kvs[gx, gy, tok : tok + 16, 128:256] = jnp.zeros((16, 128), BF16)
            factor = jnp.transpose(jnp.broadcast_to(factor, (tok, 128)))
            everything = pl.ds(0, tok)
            key = self.total(t, c, range(3), everything, slice(0, 128)) * factor
            kvs[gx, gy, 0:tok, 0:128] = rotate(key, cosines[band, :], sines[band, :]).astype(BF16)
            value = self.total(t, c, range(3), everything, slice(128, 256)) * factor
            kvs[gx, gy, 0:tok, 128:256] = value.astype(BF16)

    query = QueryReduction(part, inbox, r_send, r_recv)
    keyval = KeyValueReduction(part_kv, inbox_kv, r_kv_send, r_kv_recv)

    def compute(t):
        xx, zz = query.place(t)
        p = lookup(t, [s[2] for s in STEPS])
        band = pl.ds(pl.multiple_of(p * part_tok, part_tok), part_tok)
        lhs = rows[pl.ds(2 * xx, 2), zz, band].reshape(tok, kdim)
        for n0 in range(0, n_q, 256):
            c_tile = jnp.dot(lhs, w[:, n0 : n0 + 256], preferred_element_type=F32).astype(BF16)
            part[t, 0, :, n0 : n0 + 256] = c_tile[:part_tok]
            part[t, 1, :, n0 : n0 + 256] = c_tile[part_tok:]
        query.first(t)

    def spread_factor(zz):
        pieces = kvs[gx, zz, tok : tok + 16, 0:128].astype(F32)
        factor = jnp.sum(jnp.where(short_row < 3, pieces, 0.0), axis=0, keepdims=True)
        band = pl.ds(pl.multiple_of(zz * tok, tok), tok)
        factors[band, :] = jnp.transpose(jnp.broadcast_to(factor, (tok, 128)))

    wide_lane = lax.broadcasted_iota(jnp.int32, (2 * tok, 128), 1)

    def kv_product(k):
        xx, zz = keyval.place(k)
        pair = pl.ds(2 * xx, 2)
        squares = jnp.zeros((2 * tok, 128), F32)
        for k0 in range(0, kdim, 128):
            some = rows[pair, zz, :, k0 : k0 + 128].reshape(2 * tok, 128).astype(F32)
            squares = squares + some * some
        square = jnp.sum(squares, axis=1, keepdims=True)
        high = square.astype(BF16).astype(F32)
        spread = jnp.where(wide_lane == 0, high, jnp.where(wide_lane == 1, square - high, 0.0))
        lhs = rows[pair, zz].reshape(2 * tok, kdim)
        tile = lax.dot_general(lhs, w_kv[...], (((1,), (1,)), ((), ())), preferred_element_type=F32).astype(BF16)
        for c in (0, 1):
            part_kv[2 * k + c, 0:tok, :] = tile[c * tok : (c + 1) * tok]
            turned = jnp.transpose(spread[c * tok : (c + 1) * tok])
            part_kv[2 * k + c, tok : tok + 16, 0:128] = turned[0:16].astype(BF16)
            part_kv[2 * k + c, tok : tok + 16, 128:256] = jnp.zeros((16, 128), BF16)
        keyval.first(k)

    def stages(stage, begin, end=N_STEPS):
        lax.fori_loop(begin, end, lambda t, carry: (stage(t), carry)[1], 0)

    named = {
        "kv_near": lambda: [kv_gather.arrive(*pieces) for pieces in KV_EVENTS[:4]],
        "kv_far": lambda: [kv_gather.arrive(*pieces) for pieces in KV_EVENTS[4:5]],
        "weights_near": weights_near,
        "weights_far": weights_far,
        "kv_products": lambda: stages(kv_product, 0, 4),
        "kv_relay": lambda: stages(keyval.relay, 0, 4),
        "kv_owner": lambda: (stages(keyval.owner, 0, 4), kv_gather.begin()),
        "kv_plane": lambda: stages(keyval.plane, 0, 4),
    }

    def slot(n, carry):
        for k, (events, _, _, _) in enumerate(SLOTS):
            if events:

                @pl.when(n == k)
                def _():
                    for event in events:
                        if isinstance(event, str) and event != "weights_own":
                            named[event]()
                    pieces = [event for event in events if not isinstance(event, str)]
                    if pieces:
                        gather.arrive(*pieces)
                    if "weights_own" in events:
                        weights_own()

        @pl.when(n < N_STEPS // 2)
        def _():
            received(rows.at[0, 0], a_side_recv.at[n])

        for at_slot, stage in ((1, compute), (2, query.relay), (3, query.plane)):
            counts = [s[at_slot] for s in SLOTS]
            stages(stage, lookup(n, [0] + counts[:-1]), lookup(n, counts))
        return carry

    lax.fori_loop(0, len(SLOTS), slot, 0)

    for event in KV_EVENTS[5:12]:
        kv_gather.arrive(*event)
    stages(spread_factor, 0, 4)
    stages(query.owner, 0)
    q_out = pltpu.make_async_copy(q_ref, q_hbm, out_sem.at[0])
    q_out.start()
    for event in KV_EVENTS[12:]:
        kv_gather.arrive(*event)
    received(kvs.at[:, :, pl.ds(0, tok // 2)], k_side_recv.at[0])
    slots = kv_ref.shape[0]
    for s in range(slots):
        head = order_ref[slots * gy + s]
        for g in range(4):
            kv_ref[s, g * tok : (g + 1) * tok, :] = kvs[head, g, 0:tok, :]
    kv_out = pltpu.make_async_copy(kv_ref, kv_hbm, out_sem.at[1])
    kv_out.start()

    gather.finish()
    kv_gather.finish()

    left(wkv.at[pl.ds(0, 3)], w_send)
    owned = N_STEPS // 4
    left(part.at[pl.ds(0, N_STEPS - owned // 2)], r_send)
    left(part_kv.at[pl.ds(0, 7)], r_kv_send)
    q_out.wait()
    kv_out.wait()


def pass_on(q_in, kv_in, q_out, kv_out, q_buf, kv_buf, sems):
    takes, puts = [], []
    for n, (source, buf, target) in enumerate(((q_in, q_buf, q_out), (kv_in, kv_buf, kv_out))):
        half = buf.shape[0] // 2
        for i in (0, 1):
            piece = pl.ds(i * half, half)
            takes.append(pltpu.make_async_copy(source.at[piece], buf.at[piece], sems.at[0, n, i]))
            puts.append(pltpu.make_async_copy(buf.at[piece], target.at[piece], sems.at[1, n, i]))
    for take in takes:
        take.start()
    for take, put in zip(takes, puts):
        take.wait()
        put.start()
    for put in puts:
        put.wait()


def body(hidden_rows, norm_gain, w_query, w_keyval, positions, keyval_order):
    tok, kdim = hidden_rows.shape
    n_q, n_kv = w_query.shape[1], w_keyval.shape[1]
    n_head = 4 * n_kv
    n_tok = positions.shape[0]
    freq = np.exp((np.arange(128) // 2) * (-2.0 * math.log(rope_base) / HD)).astype(np.float32)[None, :]
    hbm = pl.BlockSpec(memory_space=pl.ANY)
    vmem = pl.BlockSpec(memory_space=pltpu.VMEM)
    dma = pltpu.SemaphoreType.DMA
    outs = (
        jax.ShapeDtypeStruct((n_tok, n_q), BF16),
        jax.ShapeDtypeStruct((2, n_tok, 2 * HD), BF16),
    )
    results = pl.pallas_call(
        fused,
        out_shape=outs,
        in_specs=[hbm, vmem, hbm, hbm, vmem, vmem, pl.BlockSpec(memory_space=pltpu.SMEM)],
        out_specs=(hbm, hbm),
        scratch_shapes=[
            pltpu.VMEM((8, 4, tok, kdim), BF16),
            pltpu.VMEM((kdim, n_q), BF16),
            pltpu.VMEM((kdim, n_q), BF16),
            pltpu.VMEM((4, n_kv, kdim), BF16),
            pltpu.VMEM((n_head, kdim), BF16),
            pltpu.VMEM((N_STEPS, 2, tok // 2, n_q), BF16),
            pltpu.VMEM((8, tok + 16, n_head), BF16),
            pltpu.VMEM((N_STEPS, 2, 3, tok // 2, n_q), BF16),
            pltpu.VMEM((4, 2, 3, tok + 16, n_head), BF16),
            pltpu.VMEM((8, 4, tok + 16, n_head), BF16),
            pltpu.VMEM((n_tok, 128), F32),
            pltpu.VMEM((n_tok, 128), F32),
            pltpu.VMEM((n_tok, 128), F32),
            dma((3,)),
            dma((2,)), dma((N_STEPS // 2,)), dma(()), dma((N_STEPS // 2,)),
            dma((2,)), dma((N_STEPS // 2,)), dma(()), dma((1,)),
            dma(()), dma((N_STEPS, 2)), dma(()), dma((4, 2)),
            dma(()), dma((2,)),
            pltpu.VMEM((n_tok, n_q), BF16),
            pltpu.VMEM((2, n_tok, 2 * HD), BF16),
            dma((2,)),
        ],
        compiler_params=pltpu.CompilerParams(
            collective_id=0, has_side_effects=True, vmem_limit_bytes=62 * 1024 * 1024
        ),
        name="fused",
    )(
        hidden_rows,
        norm_gain.reshape(1, -1),
        w_query,
        w_keyval.T,
        positions.reshape(-1, 128),
        jnp.asarray(freq),
        keyval_order,
    )
    return pl.pallas_call(
        pass_on,
        out_shape=outs,
        in_specs=[hbm, hbm],
        out_specs=(hbm, hbm),
        scratch_shapes=[pltpu.VMEM(out.shape, out.dtype) for out in outs] + [dma((2, 2, 2))],
        name="pass_on",
    )(*results)


def solution(mesh):
    in_specs = (
        P(("gx", "gy"), "gz"),
        P("gz"),
        P("gz", ("gx", "gy")),
        P("gz", ("gx", "gy")),
        P("gz"),
        P(),
    )
    out_specs = (P("gz", ("gx", "gy")), P("gy", "gz", None))
    return jax.shard_map(body, mesh=mesh, in_specs=in_specs, out_specs=out_specs, check_vma=False)
```

time: 125 us -> 116 us (0.928)
  Pallas kernels: 122 us -> 114 us
    pallas_call x1, Pallas kernels: 120 us -> 112 us  [body(): pl.pallas_call(fused, out_shape=outs, in_specs=[hbm, vmem, hbm, hbm, vmem...]
where the time goes in v3:
time: 116 us
  Pallas kernels  114 us (98%)
  local copies, waits for them, and re-layouts  1.29 us (1%)
    pallas_call x1, Pallas kernels, body(): pl.pallas_call(fused, out_shape=outs, in_specs=[hbm, vmem, hbm, hbm, vmem...  112 us

profile of v3, /device:TPU:1, one launch (start us, length us, event | category | flops | bytes accessed | tf_op | source)
XLA Modules:
  0.0 115.6 jit_solution(14325036921875149780)
XLA Ops:
  0.6 1.3 %reshape.10.gain_ref = bf16[1,2048]{1,0:T(2,128)(2,1)} reshape(bf16[2048]{0:T(1024)(128)(2,1)} %param.8) | data formatting | bytes 8192 | tf_op jit(solution)/shard_map/reshape | solution.py:540
  1.9 111.7 %fused.1 = (bf16[512,512]{1,0:T(8,128)(2,1)}, bf16[2,512,256]{2,1,0:T(8,128)(2,1)}) custom-call(bf16[128,2048]{1,0:T(8,128)(2,1)} %h_hbm.1, bf16[1,2048]{1,0:T(2,128)(2,1)} %reshape.10.gain_ref, bf16[2048,512]{1,0:T(8,128)(2,1)} %wq_hbm.1, bf16[64,2048]{1,0:T(8,128)(2,1)} %bitcast.2, s32[4,128]{1,0:T(4,128)} %bitcast.3, f32[1,128]{1,0:T(1,128)} %constant.2.clone.freq_ref, ...), custom_call_target="tpu_custom_call" | custom-call | tf_op jit(solution)/shard_map/fused/pallas_call | solution.py:506
  113.6 2.0 %pass_on.1 = (bf16[512,512]{1,0:T(8,128)(2,1)}, bf16[2,512,256]{2,1,0:T(8,128)(2,1)}) custom-call(bf16[512,512]{1,0:T(8,128)(2,1)} %get-tuple-element.4.q_in, bf16[2,512,256]{2,1,0:T(8,128)(2,1)} %get-tuple-element.5.kv_in), custom_call_target="tpu_custom_call" | custom-call | tf_op jit(solution)/shard_map/pass_on/pallas_call | solution.py:547

commit v4 on v3

--- a/solution.py
+++ b/solution.py
@@ -32,8 +32,8 @@
     [(L, R, 1), (R, L, 0)],
     [(L, L, 1), (R, R, 0)],
     [(O, F, 0), (O, F, 1)],
-    [(L, R, 0), (R, L, 1)],
-    ["weights_near", (F, L, 0), (F, R, 1)],
+    ["weights_near", (L, R, 0), (R, L, 1)],
+    [(F, L, 0), (F, R, 1)],
     [(L, F, 0), (R, F, 1)],
     ["weights_far", "kv_products", (L, F, 1), (R, F, 0)],
     ["kv_relay", (F, R, 0), (F, L, 1)],
@@ -43,17 +43,19 @@
 N_STEPS = len(STEPS)
 PAIR = {step: n // 2 for n, step in enumerate(STEPS)}
 
-SLOTS = [(events, 2 * n + 2, max(2 * n - 2, 0), max(2 * n - 6, 0)) for n, events in enumerate(ARRIVALS)] + [
-    (["kv_owner"], 32, 32, 28),
-    (["kv_near"], 32, 32, 32),
+SLOTS = [(events, max(2 * n, 2), max(2 * n - 4, 0), max(2 * n - 8, 0)) for n, events in enumerate(ARRIVALS)] + [
+    ([], 32, 26, 22),
+    (["kv_owner"], 32, 30, 26),
+    (["kv_near"], 32, 32, 28),
     (["kv_far"], 32, 32, 32),
 ]
 KV_STEPS = (O, L, R, F)
 
 KV_EVENTS = [
     [(O, L, 0), (O, R, 1)], [(L, O, 0), (R, O, 1)], [(O, L, 1), (O, R, 0)], [(L, O, 1), (R, O, 0)], [(O, F, 0), (O, F, 1)],
-    [(F, O, 0), (F, O, 1)], [(L, L, 0), (R, R, 1)], [(L, R, 1), (R, L, 0)], [(L, L, 1), (R, R, 0)], [(L, R, 0), (R, L, 1)],
-    [(F, L, 0), (F, R, 1)], [(L, F, 0), (R, F, 1)], [(L, F, 1), (R, F, 0)], [(F, R, 0), (F, L, 1)], [(F, F, 0), (F, F, 1)],
+    [(L, L, 0), (R, R, 1)], [(L, R, 0), (R, L, 1)], [(L, F, 0), (R, F, 1)],
+    [(F, O, 0), (F, O, 1)], [(L, R, 1), (R, L, 0)], [(L, L, 1), (R, R, 0)], [(F, L, 0), (F, R, 1)],
+    [(L, F, 1), (R, F, 0)], [(F, R, 0), (F, L, 1)], [(F, F, 0), (F, F, 1)],
 ]
 
 
@@ -203,7 +205,7 @@
     def weights_far():
         received(wkv.at[pl.ds(0, 2)], w_recv.at[1])
         for g in range(4):
-            w_kv[g * n_kv : (g + 1) * n_kv, :] = (wkv[g].astype(F32) * gain_ref[...].astype(F32)).astype(BF16)
+            w_kv[g * n_kv : (g + 1) * n_kv, :] = (wkv[g].astype(F32) * gain_ref[...].astype(F32)[None, :]).astype(BF16)
 
     loads[0].wait()
     loads[2].wait()
@@ -217,7 +219,7 @@
 
     for i in range(kdim // side_len):
         band = slice(i * side_len, (i + 1) * side_len)
-        gain = jnp.broadcast_to(gain_ref[:, band].astype(F32), (side_len, side_len))
+        gain = jnp.broadcast_to(gain_ref[band].astype(F32)[None, :], (side_len, side_len))
         diagonal = jnp.where(row_id == lane, gain, 0.0).astype(BF16)
         w[band, 0:n_q] = jnp.dot(diagonal, wq[band, :], preferred_element_type=F32).astype(BF16)
 
@@ -370,6 +372,11 @@
     def compute(t):
         xx, zz = query.place(t)
         p = lookup(t, [s[2] for s in STEPS])
+
+        @pl.when(t % 2 == 0)
+        def _():
+            received(rows.at[0, 0], a_side_recv.at[t // 2])
+
         band = pl.ds(pl.multiple_of(p * part_tok, part_tok), part_tok)
         lhs = rows[pl.ds(2 * xx, 2), zz, band].reshape(tok, kdim)
         for n0 in range(0, n_q, 256):
@@ -378,7 +385,8 @@
             part[t, 1, :, n0 : n0 + 256] = c_tile[part_tok:]
         query.first(t)
 
-    def spread_factor(zz):
+    def spread_factor(oz):
+        zz = (zh + oz) % 4
         pieces = kvs[gx, zz, tok : tok + 16, 0:128].astype(F32)
         factor = jnp.sum(jnp.where(short_row < 3, pieces, 0.0), axis=0, keepdims=True)
         band = pl.ds(pl.multiple_of(zz * tok, tok), tok)
@@ -410,7 +418,7 @@
 
     named = {
         "kv_near": lambda: [kv_gather.arrive(*pieces) for pieces in KV_EVENTS[:4]],
-        "kv_far": lambda: [kv_gather.arrive(*pieces) for pieces in KV_EVENTS[4:5]],
+        "kv_far": lambda: kv_gather.arrive(*KV_EVENTS[4]),
         "weights_near": weights_near,
         "weights_far": weights_far,
         "kv_products": lambda: stages(kv_product, 0, 4),
@@ -434,10 +442,6 @@
                     if "weights_own" in events:
                         weights_own()
 
-        @pl.when(n < N_STEPS // 2)
-        def _():
-            received(rows.at[0, 0], a_side_recv.at[n])
-
         for at_slot, stage in ((1, compute), (2, query.relay), (3, query.plane)):
             counts = [s[at_slot] for s in SLOTS]
             stages(stage, lookup(n, [0] + counts[:-1]), lookup(n, counts))
@@ -445,13 +449,28 @@
 
     lax.fori_loop(0, len(SLOTS), slot, 0)
 
-    for event in KV_EVENTS[5:12]:
-        kv_gather.arrive(*event)
-    stages(spread_factor, 0, 4)
-    stages(query.owner, 0)
+    def owner_near(t):
+        @pl.when(lookup(t, [int(s[1] != F) for s in STEPS]) == 1)
+        def _():
+            query.owner(t)
+
+    def owner_far(t):
+        @pl.when(lookup(t, [int(s[1] == F) for s in STEPS[:28]] + [1] * 4) == 1)
+        def _():
+            query.owner(t)
+
+    kv_gather.arrive(*KV_EVENTS[5])
+    for oz in (O, L, R):
+        spread_factor(oz)
+    stages(owner_near, 0, 16)
+    kv_gather.arrive(*KV_EVENTS[6])
+    stages(owner_near, 16, 28)
+    kv_gather.arrive(*KV_EVENTS[7])
+    spread_factor(F)
+    stages(owner_far, 0)
     q_out = pltpu.make_async_copy(q_ref, q_hbm, out_sem.at[0])
     q_out.start()
-    for event in KV_EVENTS[12:]:
+    for event in KV_EVENTS[8:]:
         kv_gather.arrive(*event)
     received(kvs.at[:, :, pl.ds(0, tok // 2)], k_side_recv.at[0])
     slots = kv_ref.shape[0]
@@ -537,7 +556,7 @@
         name="fused",
     )(
         hidden_rows,
-        norm_gain.reshape(1, -1),
+        norm_gain,
         w_query,
         w_keyval.T,
         positions.reshape(-1, 128),

time: 116 us -> 110 us (0.948)
  Pallas kernels: 114 us -> 109 us
  local copies, waits for them, and re-layouts: 1.29 us -> 0 us
    pallas_call x1, Pallas kernels: 112 us -> 107 us  [body(): pl.pallas_call(fused, out_shape=outs, in_specs=[hbm, vmem, hbm, hbm, vmem...]
    reshape x1 -> x0, local copies, waits for them, and re-layouts: 1.29 us -> none  [body(): norm_gain.reshape(1, -1)]
where the time goes in v4:
time: 110 us; the launch traced here: 109 us
  Pallas kernels  109 us (99%)
    pallas_call x1, Pallas kernels, body(): pl.pallas_call(fused, out_shape=outs, in_specs=[hbm, vmem, hbm, hbm, vmem...  107 us

profile of v4, /device:TPU:1, one launch (start us, length us, event | category | flops | bytes accessed | tf_op | source)
XLA Modules:
  0.0 109.4 jit_solution(18221220289189341985)
XLA Ops:
  0.6 106.8 %fused.1 = (bf16[512,512]{1,0:T(8,128)(2,1)}, bf16[2,512,256]{2,1,0:T(8,128)(2,1)}) custom-call(bf16[128,2048]{1,0:T(8,128)(2,1)} %h_hbm.1, bf16[2048]{0:T(1024)(128)(2,1)} %gain_ref.1, bf16[2048,512]{1,0:T(8,128)(2,1)} %wq_hbm.1, bf16[64,2048]{1,0:T(8,128)(2,1)} %bitcast.2, s32[4,128]{1,0:T(4,128)} %bitcast.3, f32[1,128]{1,0:T(1,128)} %constant.2.clone.freq_ref, ...), custom_call_target="tpu_custom_call" | custom-call | tf_op jit(solution)/shard_map/fused/pallas_call | solution.py:525
  107.4 2.0 %pass_on.1 = (bf16[512,512]{1,0:T(8,128)(2,1)}, bf16[2,512,256]{2,1,0:T(8,128)(2,1)}) custom-call(bf16[512,512]{1,0:T(8,128)(2,1)} %get-tuple-element.4.q_in, bf16[2,512,256]{2,1,0:T(8,128)(2,1)} %get-tuple-element.5.kv_in), custom_call_target="tpu_custom_call" | custom-call | tf_op jit(solution)/shard_map/pass_on/pallas_call | solution.py:566

commit v5 on v4

--- a/solution.py
+++ b/solution.py
@@ -29,34 +29,41 @@
     [(F, O, 0), (F, O, 1)],
     [(L, L, 0), (R, R, 1)],
     [(O, L, 1), (O, R, 0)],
-    [(L, R, 1), (R, L, 0)],
+    ["weights_near", (L, R, 1), (R, L, 0)],
     [(L, L, 1), (R, R, 0)],
+    [(L, R, 0), (R, L, 1)],
+    ["weights_far", "kv_products", (F, L, 0), (F, R, 1)],
     [(O, F, 0), (O, F, 1)],
-    ["weights_near", (L, R, 0), (R, L, 1)],
-    [(F, L, 0), (F, R, 1)],
-    [(L, F, 0), (R, F, 1)],
-    ["weights_far", "kv_products", (L, F, 1), (R, F, 0)],
     ["kv_relay", (F, R, 0), (F, L, 1)],
-    ["kv_plane", (F, F, 0), (F, F, 1)],
+    ["kv_plane", (L, F, 0), (R, F, 1)],
+    ["kv_owner", (L, F, 1), (R, F, 0)],
+    ["kv_z", (F, F, 0), (F, F, 1)],
 ]
 STEPS = [(O, O, 0), (O, O, 1)] + [e for events in ARRIVALS for e in events if not isinstance(e, str)]
 N_STEPS = len(STEPS)
 PAIR = {step: n // 2 for n, step in enumerate(STEPS)}
 
-SLOTS = [(events, max(2 * n, 2), max(2 * n - 4, 0), max(2 * n - 8, 0)) for n, events in enumerate(ARRIVALS)] + [
-    ([], 32, 26, 22),
-    (["kv_owner"], 32, 30, 26),
-    (["kv_near"], 32, 32, 28),
-    (["kv_far"], 32, 32, 32),
+def slot_counts(n):
+    lag = 4 if n < 11 else 2
+    return max(2 * n, 2), max(2 * n - lag, 0), max(2 * n - 2 * lag, 0)
+
+
+SLOTS = [(events, *slot_counts(n)) for n, events in enumerate(ARRIVALS[:-1])] + [
+    ([], 30, 28, 26),
+    (ARRIVALS[-1], 32, 30, 28),
+    (["kv_far"], 32, 32, 30),
+    (["kv_x", "owner_early"], 32, 32, 32),
 ]
 KV_STEPS = (O, L, R, F)
 
-KV_EVENTS = [
-    [(O, L, 0), (O, R, 1)], [(L, O, 0), (R, O, 1)], [(O, L, 1), (O, R, 0)], [(L, O, 1), (R, O, 0)], [(O, F, 0), (O, F, 1)],
-    [(L, L, 0), (R, R, 1)], [(L, R, 0), (R, L, 1)], [(L, F, 0), (R, F, 1)],
-    [(F, O, 0), (F, O, 1)], [(L, R, 1), (R, L, 0)], [(L, L, 1), (R, R, 0)], [(F, L, 0), (F, R, 1)],
-    [(L, F, 1), (R, F, 0)], [(F, R, 0), (F, L, 1)], [(F, F, 0), (F, F, 1)],
+KV_Z = [[(O, L, 0), (O, R, 1)], [(O, L, 1), (O, R, 0)]]
+KV_FAR = [[(O, F, 0), (O, F, 1)], [(L, O, 0), (R, O, 1)]]
+KV_X = [[(L, O, 1), (R, O, 0)], [(L, L, 0), (R, R, 1)], [(L, R, 0), (R, L, 1)]]
+KV_LAST = [
+    [(L, F, 0), (R, F, 1)], [(F, O, 0), (F, O, 1)], [(L, R, 1), (R, L, 0)], [(L, L, 1), (R, R, 0)],
+    [(F, L, 0), (F, R, 1)], [(L, F, 1), (R, F, 0)], [(F, R, 0), (F, L, 1)], [(F, F, 0), (F, F, 1)],
 ]
+EARLY = 24
 
 
 def lookup(t, values):
@@ -141,13 +148,15 @@
             for p in (0, 1):
                 self.side(O, O, p)
 
-        def arrive(self, *pieces):
+        def forward_z(self):
+            self.push(O, L, 0, O, F, z_up)
+            self.push(O, R, 1, O, F, z_down)
+
+        def arrive(self, *pieces, late=False):
             whole = self.buf.at[0, 0] if pieces[0][0] == O else self.buf.at[0, 0, pl.ds(0, tok)]
             received(whole, self.recv.at[PAIR[pieces[0]]])
-            if (O, L, 0) in pieces:
-                self.push(O, L, 0, O, F, z_up)
-            if (O, R, 1) in pieces:
-                self.push(O, R, 1, O, F, z_down)
+            if pieces[0] == (O, L, 0) and not late:
+                self.forward_z()
             for ox, oz, p in pieces:
                 if ox == O:
                     self.push(O, oz, p, L, oz, x_up)
@@ -201,6 +210,7 @@
         received(wkv.at[0], w_recv.at[0])
         for args in weights_sent[4:]:
             weights_copy(*args).start()
+        gather.forward_z()
 
     def weights_far():
         received(wkv.at[pl.ds(0, 2)], w_recv.at[1])
@@ -417,8 +427,10 @@
         lax.fori_loop(begin, end, lambda t, carry: (stage(t), carry)[1], 0)
 
     named = {
-        "kv_near": lambda: [kv_gather.arrive(*pieces) for pieces in KV_EVENTS[:4]],
-        "kv_far": lambda: kv_gather.arrive(*KV_EVENTS[4]),
+        "kv_z": lambda: ([kv_gather.arrive(*pieces) for pieces in KV_Z], [spread_factor(oz) for oz in (O, L, R)]),
+        "kv_far": lambda: ([kv_gather.arrive(*pieces) for pieces in KV_FAR], spread_factor(F)),
+        "kv_x": lambda: [kv_gather.arrive(*pieces) for pieces in KV_X],
+        "owner_early": lambda: stages(owner_early, 0, EARLY),
         "weights_near": weights_near,
         "weights_far": weights_far,
         "kv_products": lambda: stages(kv_product, 0, 4),
@@ -427,6 +439,18 @@
         "kv_plane": lambda: stages(keyval.plane, 0, 4),
     }
 
+    is_late = [int(s[1] == F) for s in STEPS[:EARLY]] + [1] * (N_STEPS - EARLY)
+
+    def owner_early(t):
+        @pl.when(lookup(t, is_late) == 0)
+        def _():
+            query.owner(t)
+
+    def owner_late(t):
+        @pl.when(lookup(t, is_late) == 1)
+        def _():
+            query.owner(t)
+
     def slot(n, carry):
         for k, (events, _, _, _) in enumerate(SLOTS):
             if events:
@@ -438,7 +462,7 @@
                             named[event]()
                     pieces = [event for event in events if not isinstance(event, str)]
                     if pieces:
-                        gather.arrive(*pieces)
+                        gather.arrive(*pieces, late=True)
                     if "weights_own" in events:
                         weights_own()
 
@@ -459,18 +483,11 @@
         def _():
             query.owner(t)
 
-    kv_gather.arrive(*KV_EVENTS[5])
-    for oz in (O, L, R):
-        spread_factor(oz)
-    stages(owner_near, 0, 16)
-    kv_gather.arrive(*KV_EVENTS[6])
-    stages(owner_near, 16, 28)
-    kv_gather.arrive(*KV_EVENTS[7])
-    spread_factor(F)
-    stages(owner_far, 0)
+    kv_gather.arrive(*KV_LAST[0])
+    stages(owner_late, 0)
     q_out = pltpu.make_async_copy(q_ref, q_hbm, out_sem.at[0])
     q_out.start()
-    for event in KV_EVENTS[8:]:
+    for event in KV_LAST[1:]:
         kv_gather.arrive(*event)
     received(kvs.at[:, :, pl.ds(0, tok // 2)], k_side_recv.at[0])
     slots = kv_ref.shape[0]

time: 110 us -> 108 us (0.982)
  Pallas kernels: 109 us -> 106 us
    pallas_call x1, Pallas kernels: 107 us -> 104 us  [body(): pl.pallas_call(fused, out_shape=outs, in_specs=[hbm, vmem, hbm, hbm, vmem...]
where the time goes in v5:
time: 108 us; the launch traced here: 107 us
  Pallas kernels  106 us (98%)
    pallas_call x1, Pallas kernels, body(): pl.pallas_call(fused, out_shape=outs, in_specs=[hbm, vmem, hbm, hbm, vmem...  104 us

profile of v5, /device:TPU:1, one launch (start us, length us, event | category | flops | bytes accessed | tf_op | source)
XLA Modules:
  0.0 106.7 jit_solution(20336627953063370)
XLA Ops:
  0.6 104.0 %fused.1 = (bf16[512,512]{1,0:T(8,128)(2,1)}, bf16[2,512,256]{2,1,0:T(8,128)(2,1)}) custom-call(bf16[128,2048]{1,0:T(8,128)(2,1)} %h_hbm.1, bf16[2048]{0:T(1024)(128)(2,1)} %gain_ref.1, bf16[2048,512]{1,0:T(8,128)(2,1)} %wq_hbm.1, bf16[64,2048]{1,0:T(8,128)(2,1)} %bitcast.2, s32[4,128]{1,0:T(4,128)} %bitcast.3, f32[1,128]{1,0:T(1,128)} %constant.2.clone.freq_ref, ...), custom_call_target="tpu_custom_call" | custom-call | tf_op jit(solution)/shard_map/fused/pallas_call | solution.py:542
  104.7 2.0 %pass_on.1 = (bf16[512,512]{1,0:T(8,128)(2,1)}, bf16[2,512,256]{2,1,0:T(8,128)(2,1)}) custom-call(bf16[512,512]{1,0:T(8,128)(2,1)} %get-tuple-element.4.q_in, bf16[2,512,256]{2,1,0:T(8,128)(2,1)} %get-tuple-element.5.kv_in), custom_call_target="tpu_custom_call" | custom-call | tf_op jit(solution)/shard_map/pass_on/pallas_call | solution.py:583

commit v6 on v5

--- a/solution.py
+++ b/solution.py
@@ -37,20 +37,21 @@
     ["kv_relay", (F, R, 0), (F, L, 1)],
     ["kv_plane", (L, F, 0), (R, F, 1)],
     ["kv_owner", (L, F, 1), (R, F, 0)],
-    ["kv_z", (F, F, 0), (F, F, 1)],
+    [(F, F, 0), (F, F, 1)],
 ]
 STEPS = [(O, O, 0), (O, O, 1)] + [e for events in ARRIVALS for e in events if not isinstance(e, str)]
 N_STEPS = len(STEPS)
 PAIR = {step: n // 2 for n, step in enumerate(STEPS)}
 
 def slot_counts(n):
-    lag = 4 if n < 11 else 2
+    lag = 4 if n < 13 else 2
     return max(2 * n, 2), max(2 * n - lag, 0), max(2 * n - 2 * lag, 0)
 
 
 SLOTS = [(events, *slot_counts(n)) for n, events in enumerate(ARRIVALS[:-1])] + [
-    ([], 30, 28, 26),
-    (ARRIVALS[-1], 32, 30, 28),
+    ([], 30, 26, 24),
+    (ARRIVALS[-1], 30, 28, 26),
+    (["kv_z"], 32, 30, 28),
     (["kv_far"], 32, 32, 30),
     (["kv_x", "owner_early"], 32, 32, 32),
 ]
@@ -102,8 +103,7 @@
         pltpu.make_async_copy(wq_hbm, wq, load_sem.at[1]),
         pltpu.make_async_copy(wkv_hbm, wkv.at[gy], load_sem.at[2]),
     ]
-    for load in loads:
-        load.start()
+    loads[0].start()
 
     barrier = pltpu.get_barrier_semaphore()
     peers = [
@@ -218,11 +218,13 @@
             w_kv[g * n_kv : (g + 1) * n_kv, :] = (wkv[g].astype(F32) * gain_ref[...].astype(F32)[None, :]).astype(BF16)
 
     loads[0].wait()
-    loads[2].wait()
+    loads[1].start()
+    loads[2].start()
     pl.semaphore_wait(barrier, len(peers))
     gather.begin()
 
     loads[1].wait()
+    loads[2].wait()
     side_len = 128
     row_id = lax.broadcasted_iota(jnp.int32, (side_len, side_len), 0)
     lane = lax.broadcasted_iota(jnp.int32, (side_len, side_len), 1)

time: 108 us -> 106 us (0.981)
  no operation moved by 1% of the time
where the time goes in v6:
time: 106 us
  Pallas kernels  105 us (99%)
    pallas_call x1, Pallas kernels, body(): pl.pallas_call(fused, out_shape=outs, in_specs=[hbm, vmem, hbm, hbm, vmem...  103 us

profile of v6, /device:TPU:1, one launch (start us, length us, event | category | flops | bytes accessed | tf_op | source)
XLA Modules:
  0.0 105.7 jit_solution(12124974170176420567)
XLA Ops:
  0.6 103.0 %fused.1 = (bf16[512,512]{1,0:T(8,128)(2,1)}, bf16[2,512,256]{2,1,0:T(8,128)(2,1)}) custom-call(bf16[128,2048]{1,0:T(8,128)(2,1)} %h_hbm.1, bf16[2048]{0:T(1024)(128)(2,1)} %gain_ref.1, bf16[2048,512]{1,0:T(8,128)(2,1)} %wq_hbm.1, bf16[64,2048]{1,0:T(8,128)(2,1)} %bitcast.2, s32[4,128]{1,0:T(4,128)} %bitcast.3, f32[1,128]{1,0:T(1,128)} %constant.2.clone.freq_ref, ...), custom_call_target="tpu_custom_call" | custom-call | tf_op jit(solution)/shard_map/fused/pallas_call | solution.py:544
  103.7 2.0 %pass_on.1 = (bf16[512,512]{1,0:T(8,128)(2,1)}, bf16[2,512,256]{2,1,0:T(8,128)(2,1)}) custom-call(bf16[512,512]{1,0:T(8,128)(2,1)} %get-tuple-element.4.q_in, bf16[2,512,256]{2,1,0:T(8,128)(2,1)} %get-tuple-element.5.kv_in), custom_call_target="tpu_custom_call" | custom-call | tf_op jit(solution)/shard_map/pass_on/pallas_call | solution.py:585

commit v7 on v6

--- a/solution.py
+++ b/solution.py
@@ -74,7 +74,7 @@
 def fused(
     h_hbm, gain_ref, wq_hbm, wkv_hbm, pos_ref, freq_ref, order_ref,
     q_hbm, kv_hbm,
-    rows, wq, w, wkv, w_kv, part, part_kv, inbox, inbox_kv, kvs, factors, cosines, sines,
+    rows, wq, w, wkv, w_kv, part, part_kv, inbox, inbox_kv, kvs, cosines, sines,
     load_sem, a_send, a_recv, a_side_send, a_side_recv,
     k_send, k_recv, k_side_send, k_side_recv, r_send, r_recv, r_kv_send, r_kv_recv,
     w_send, w_recv, q_ref, kv_ref, out_sem,
@@ -338,10 +338,10 @@
 
         def store(self, t, c, zz):
             band = pl.ds(pl.multiple_of(zz * tok + self.rows_of(t), part_tok), part_tok)
-            cos_t, sin_t, factor = cosines[band, :], sines[band, :], factors[band, :]
+            cos_t, sin_t = cosines[band, :], sines[band, :]
             for n0 in range(0, n_q, 128):
                 cols = slice(n0, n0 + 128)
-                value = self.total(t, c, range(3), slice(None), cols) * factor
+                value = self.total(t, c, range(3), slice(None), cols)
                 q_ref[band, cols] = rotate(value, cos_t, sin_t).astype(BF16)
 
     class KeyValueReduction(Reduction):
@@ -402,7 +402,9 @@
         pieces = kvs[gx, zz, tok : tok + 16, 0:128].astype(F32)
         factor = jnp.sum(jnp.where(short_row < 3, pieces, 0.0), axis=0, keepdims=True)
         band = pl.ds(pl.multiple_of(zz * tok, tok), tok)
-        factors[band, :] = jnp.transpose(jnp.broadcast_to(factor, (tok, 128)))
+        factor = jnp.transpose(jnp.broadcast_to(factor, (tok, 128)))
+        cosines[band, :] = cosines[band, :] * factor
+        sines[band, :] = sines[band, :] * factor
 
     wide_lane = lax.broadcasted_iota(jnp.int32, (2 * tok, 128), 1)
 
@@ -557,7 +559,6 @@
             pltpu.VMEM((N_STEPS, 2, 3, tok // 2, n_q), BF16),
             pltpu.VMEM((4, 2, 3, tok + 16, n_head), BF16),
             pltpu.VMEM((8, 4, tok + 16, n_head), BF16),
-            pltpu.VMEM((n_tok, 128), F32),
             pltpu.VMEM((n_tok, 128), F32),
             pltpu.VMEM((n_tok, 128), F32),
             dma((3,)),

time: 106 us -> 106 us (level)
  no operation moved by 1% of the time
where the time goes in v7:
time: 106 us
  Pallas kernels  105 us (99%)
    pallas_call x1, Pallas kernels, body(): pl.pallas_call(fused, out_shape=outs, in_specs=[hbm, vmem, hbm, hbm, vmem...  103 us

profile of v7, /device:TPU:1, one launch (start us, length us, event | category | flops | bytes accessed | tf_op | source)
XLA Modules:
  0.0 105.7 jit_solution(2367830272295418100)
XLA Ops:
  0.6 103.0 %fused.1 = (bf16[512,512]{1,0:T(8,128)(2,1)}, bf16[2,512,256]{2,1,0:T(8,128)(2,1)}) custom-call(bf16[128,2048]{1,0:T(8,128)(2,1)} %h_hbm.1, bf16[2048]{0:T(1024)(128)(2,1)} %gain_ref.1, bf16[2048,512]{1,0:T(8,128)(2,1)} %wq_hbm.1, bf16[64,2048]{1,0:T(8,128)(2,1)} %bitcast.2, s32[4,128]{1,0:T(4,128)} %bitcast.3, f32[1,128]{1,0:T(1,128)} %constant.2.clone.freq_ref, ...), custom_call_target="tpu_custom_call" | custom-call | tf_op jit(solution)/shard_map/fused/pallas_call | solution.py:546
  103.7 2.0 %pass_on.1 = (bf16[512,512]{1,0:T(8,128)(2,1)}, bf16[2,512,256]{2,1,0:T(8,128)(2,1)}) custom-call(bf16[512,512]{1,0:T(8,128)(2,1)} %get-tuple-element.4.q_in, bf16[2,512,256]{2,1,0:T(8,128)(2,1)} %get-tuple-element.5.kv_in), custom_call_target="tpu_custom_call" | custom-call | tf_op jit(solution)/shard_map/pass_on/pallas_call | solution.py:586
